TPU v7x, 32 devices: a whole 2x2x4 slice. The times are simulated.
32 devices in a mesh: dp: 4 (over y, x), ep: 8 (over z, core).
Axes of the slice: x: 2, y: 2, z: 4, core: 2. Of those that a mesh axis runs over, the one named last changes fastest.
Arguments:
- tokens: bfloat16 [4096, 7168], P(('dp', 'ep')), may hold values from -6 to 6
- out_grad: bfloat16 [4096, 7168], P(('dp', 'ep')), may hold values from -3 to 3
- route_weight: float32 [4096, 1], P(('dp', 'ep')), may hold values from 0.2 to 1
- expert_ids: int32 [4096, 1], P(('dp', 'ep')), may hold values from 0 to 1
- w_gate: bfloat16 [1024, 14336], P('dp', 'ep'), may hold values from -0.0625 to 0.0625
- w_up: bfloat16 [1024, 14336], P('dp', 'ep'), may hold values from -0.0625 to 0.0625
- w_down: bfloat16 [1024, 14336], P('dp', 'ep'), may hold values from -0.1875 to 0.1875
Outputs:
- in_grad: bfloat16 [4096, 7168], P(('dp', 'ep'))
- grad_gate: bfloat16 [1024, 14336], P('dp', 'ep')
- grad_up: bfloat16 [1024, 14336], P('dp', 'ep')
- grad_down: bfloat16 [1024, 14336], P('dp', 'ep')
All inputs are finite; a program needn't handle non-finite values.
Results may differ from a plain program's by a relative error of at most 0.012.
Values may be sent and summed in bfloat16 or wider, within the bound.
A program may use at most 128 MiB of HBM per device.

v0:
```python
import jax
import jax.numpy as jnp
from jax import lax
from jax.experimental import pallas as pl
from jax.experimental.pallas import tpu as pltpu
from jax.sharding import PartitionSpec as P

D = 7168
GROUP = 4
TOP = 1


CONTRACT_LAST = (((1,), (1,)), ((), ()))
CONTRACT_FIRST = (((0,), (0,)), ((), ()))


def as_sent(value):

    def short(part):
        return part.astype(jnp.bfloat16) if part.dtype == jnp.float32 else part

    return jax.tree.map(short, value)


def from_partner(value, axis, distance):
    mask = 2**distance
    pairs = [(source, source ^ mask) for source in range(lax.axis_size(axis))]
    return lax.ppermute(value, axis, pairs)


def slot_tables(expert_ids, route_weight, experts, capacity):
    token_count, top_count = expert_ids.shape
    pair_count = token_count * top_count
    flat_ids = expert_ids.reshape(pair_count)
    onehot = (flat_ids[:, None] == jnp.arange(experts, dtype=jnp.int32)[None, :]).astype(jnp.int32)
    before = jnp.cumsum(onehot, axis=0) - onehot
    ranks = jnp.sum(before * onehot, axis=1)
    kept = ranks < capacity
    slots = jnp.where(kept, flat_ids * capacity + ranks, 0)
    slot_ids = jnp.arange(experts * capacity, dtype=jnp.int32)
    match = (slots[None, :] == slot_ids[:, None]) & kept[None, :]
    pair_ids = jnp.arange(pair_count, dtype=jnp.int32)
    pair_of_slot = jnp.sum(jnp.where(match, pair_ids[None, :], 0), axis=1)
    filled = jnp.any(match, axis=1)
    flat_weight = route_weight.reshape(pair_count)
    weight_of_slot = jnp.sum(jnp.where(match, flat_weight[None, :], jnp.float32(0.0)), axis=1)
    return (kept, slots, pair_of_slot // top_count, filled, weight_of_slot)


def activations(gate, up, back):
    logistic = jax.nn.sigmoid(gate)
    silu = gate * logistic
    hidden = (silu * up).astype(jnp.bfloat16)
    d_gate = (back * up * logistic * (1.0 + gate * (1.0 - logistic))).astype(jnp.bfloat16)
    d_up = (back * silu).astype(jnp.bfloat16)
    return (hidden, d_gate, d_up)


def swap(value, axis, distance):
    return from_partner(value, axis, distance)


def wide(value):
    return value.astype(jnp.float32)


def dot_last(left, right):
    return lax.dot_general(left, right, CONTRACT_LAST, preferred_element_type=jnp.float32)


def dot_first(left, right):
    return lax.dot_general(left, right, CONTRACT_FIRST, preferred_element_type=jnp.float32)


def body(tokens, out_grad, route_weight, expert_ids, w_gate, w_up, w_down):
    devices_ep = lax.axis_size("ep")
    experts = devices_ep // GROUP
    token_count = tokens.shape[0]
    capacity = 6 * GROUP * token_count * TOP // (8 * devices_ep)
    quarter = D // GROUP
    short = jnp.bfloat16
    kept, slots, token_of_slot, filled, weight_of_slot = slot_tables(
        expert_ids, route_weight, experts, capacity
    )
    other_w = tuple(swap(w, "dp", 1) for w in (w_gate, w_up, w_down))
    token_ids = jnp.arange(token_count, dtype=jnp.int32)
    pick = ((token_of_slot[:, None] == token_ids[None, :]) & filled[:, None]).astype(short)
    x_slots = jnp.dot(pick, tokens, preferred_element_type=jnp.float32).astype(short)
    d_slots = (
        jnp.dot(pick, out_grad, preferred_element_type=jnp.float32) * weight_of_slot[:, None]
    ).astype(short)

    def to_owners(rows):
        shaped = rows.reshape(experts, capacity, GROUP, quarter).transpose(0, 2, 1, 3)
        return shaped.reshape(devices_ep, capacity, quarter)

    def sent(rows):
        return lax.all_to_all(to_owners(rows), "ep", split_axis=0, concat_axis=0, tiled=True)

    row_count = devices_ep * capacity
    x_own = sent(x_slots).reshape(row_count, quarter)
    d_own = sent(d_slots).reshape(row_count, quarter)
    x_other, d_other = swap(x_own, "dp", 0), swap(d_own, "dp", 0)
    core = lax.axis_index("ep") % 2
    weights = ((w_gate, w_up, w_down), other_w)
    acts = []
    for x_rows, d_rows in ((x_own, d_own), (x_other, d_other)):
        terms = [
            jnp.concatenate(
                [dot_last(x_rows, wg), dot_last(x_rows, wu), dot_last(d_rows, wd)], axis=1
            ).astype(short)
            for wg, wu, wd in weights
        ]
        give = jnp.where(core == 0, terms[1], terms[0])
        keep = jnp.where(core == 0, terms[0], terms[1])
        pair = (wide(keep) + wide(swap(give, "ep", 0))).astype(short)
        total = wide(pair) + wide(swap(pair, "ep", 1))
        width = total.shape[1] // 3
        mine = jnp.concatenate(
            activations(total[:, :width], total[:, width : 2 * width], total[:, 2 * width :]), axis=1
        )
        theirs = swap(mine, "ep", 0)
        first = jnp.where(core == 0, mine, theirs)
        second = jnp.where(core == 0, theirs, mine)
        acts.append(
            tuple(
                tuple(half[:, piece * width : (piece + 1) * width] for piece in range(3))
                for half in (first, second)
            )
        )

    def grads(half):
        (h0, g0, u0), (h1, g1, u1) = acts[0][half], acts[1][half]
        return (
            dot_first(g0, x_own) + dot_first(g1, x_other),
            dot_first(u0, x_own) + dot_first(u1, x_other),
            dot_first(h0, d_own) + dot_first(h1, d_other),
        )

    def dx(rows):
        return sum(
            jnp.dot(acts[rows][half][1], weights[half][0], preferred_element_type=jnp.float32)
            + jnp.dot(acts[rows][half][2], weights[half][1], preferred_element_type=jnp.float32)
            for half in range(2)
        )

    dx_in = swap(dx(1).astype(short), "dp", 0)
    away = tuple(swap(term.astype(short), "dp", 1) for term in grads(1))
    expert_dx = (dx(0) + wide(dx_in)).astype(short)
    grad_gate, grad_up, grad_down = (
        (own + wide(term)).astype(short) for own, term in zip(grads(0), away)
    )
    returned = lax.all_to_all(
        expert_dx.reshape(devices_ep, capacity, quarter),
        "ep",
        split_axis=0,
        concat_axis=0,
        tiled=True,
    )
    slot_rows = (
        returned.reshape(experts, GROUP, capacity, quarter)
        .transpose(0, 2, 1, 3)
        .reshape(experts * capacity, D)
    )
    in_grad = dot_first(pick, slot_rows).astype(short)
    return (in_grad, grad_gate, grad_up, grad_down)


MESH = pl.DeviceIdType.MESH
LANES = 256


def flip(index, bit):
    size = 1 << bit
    return index + size - 2 * size * lax.rem(lax.div(index, size), 2)


def expert_kernel(
    tokens, out_grad, pick, pick_t, scale, wg, wu, wd, in_grad, grad_gate, grad_up, grad_down,
    xs, ds, slot_rows, x_all, d_all, w_all, part, got, pair, across, act, act_t,
    term_out, term_in, term_own, dx_out, dx_in, dx_own, dx_sum,
    w_local, w_send, w_recv, self_sem, x_send, x_recv, d_send, d_recv,
    fx_send, fx_recv, fd_send, fd_recv, give_send, give_recv, pair_send, pair_recv,
    act_send, act_recv, term_send, term_recv, dx_send, dx_recv, back_send, back_recv,
):
    devices_ep, capacity, quarter = dx_sum.shape
    rows = devices_ep * capacity
    hidden = wg.shape[0]
    r, s = lax.axis_index("dp"), lax.axis_index("ep")
    core = lax.rem(s, 2)
    row_mate, weight_mate = (flip(r, 0), s), (flip(r, 1), s)
    core_mate, chip_mate = (r, flip(s, 0)), (r, flip(s, 1))
    order = list(range(devices_ep - 1, 0, -1))

    def mate(mask):
        index = s
        for bit in range(mask.bit_length()):
            if mask >> bit & 1:
                index = flip(index, bit)
        return index

    barrier = pltpu.get_barrier_semaphore()
    peers = [row_mate, weight_mate]
    peers += [(r, mate(j)) for j in range(1, devices_ep)]
    for peer in peers:
        pl.semaphore_signal(barrier, inc=1, device_id=peer, device_id_type=MESH)
    pl.semaphore_wait(barrier, len(peers))

    def remote(source, target, send, recv, peer):
        copy = pltpu.make_async_remote_copy(
            src_ref=source, dst_ref=target, send_sem=send, recv_sem=recv,
            device_id=peer, device_id_type=MESH,
        )
        copy.start()
        return copy

    def local(source, target, sem):
        copy = pltpu.make_async_copy(source, target, sem)
        copy.start()
        return copy

    def owned(ref, device):
        row = pl.multiple_of(lax.div(device, GROUP) * capacity, capacity)
        column = pl.multiple_of(lax.rem(device, GROUP) * quarter, 128)
        return ref.at[pl.ds(row, capacity), pl.ds(column, quarter)]

    WIDE = 4 * 128

    def by_slots(fn):
        def one(n, carry):
            fn(pl.ds(pl.multiple_of(n * WIDE, WIDE), WIDE))
            return carry

        lax.fori_loop(0, xs.shape[1] // WIDE, one, 0)

    def fill_x(at):
        xs[:, at] = jnp.dot(
            pick[...], tokens[:, at], preferred_element_type=jnp.float32
        ).astype(jnp.bfloat16)

    def fill_d(at):
        ds[:, at] = (
            jnp.dot(pick[...], out_grad[:, at], preferred_element_type=jnp.float32) * scale[...]
        ).astype(jnp.bfloat16)

    weights = (wg, wu, wd)
    w_copies = [
        remote(w, w_all.at[1, i], w_send.at[i], w_recv.at[i], weight_mate)
        for i, w in enumerate(weights)
    ]
    own_w = [local(w, w_all.at[0, i], w_local.at[i]) for i, w in enumerate(weights)]
    x_copies, d_copies = {}, {}
    self_copies = []
    for n, (fill, copies, source, target, send, recv) in enumerate((
        (fill_x, x_copies, xs, x_all, x_send, x_recv),
        (fill_d, d_copies, ds, d_all, d_send, d_recv),
    )):
        by_slots(fill)
        for j in order:
            peer = mate(j)
            copies[j] = remote(
                owned(source, peer), target.at[0, s], send.at[j], recv.at[j], (r, peer)
            )
        self_copies.append(local(owned(source, s), target.at[0, s], self_sem.at[n]))
    passed = ([], [])

    def pass_on(n, j):
        copies, target, send, recv = (
            (x_copies, x_all, fx_send, fx_recv),
            (d_copies, d_all, fd_send, fd_recv),
        )[n]
        if j:
            copies[j].wait_recv()
        else:
            self_copies[n].wait()
        origin = mate(j)
        passed[n].append(
            remote(target.at[0, origin], target.at[1, origin], send.at[j], recv.at[j], row_mate)
        )

    def project(k, which, pieces):
        for i in pieces:
            block = (x_all if i < 2 else d_all)[k].reshape(rows, quarter)
            part[k, which, i] = dot_last(block, w_all[which, i]).astype(jnp.bfloat16)

    STEP = 48

    def by_rows(fn):
        def one(n, carry):
            fn(pl.ds(pl.multiple_of(n * STEP, STEP), STEP))
            return carry

        lax.fori_loop(0, rows // STEP, one, 0)

    give_copies, pair_copies, act_copies = {}, {}, []
    groups = ((0, 1), (2,))

    def hand_over(k, g):
        pieces = pl.ds(groups[g][0], len(groups[g]))
        give_copies[k, g] = remote(
            part.at[k, 1 - core, pieces], got.at[k, pieces],
            give_send.at[2 * k + g], give_recv.at[2 * k + g], core_mate,
        )

    def send_pair(k, g):
        give_copies[k, g].wait_recv()

        def add_pair(at):
            for i in groups[g]:
                pair[k, i, at, :] = (wide(part[k, core, i, at, :]) + wide(got[k, i, at, :])).astype(
                    jnp.bfloat16
                )

        by_rows(add_pair)
        pieces = pl.ds(groups[g][0], len(groups[g]))
        pair_copies[k, g] = remote(
            pair.at[k, pieces], across.at[k, pieces],
            pair_send.at[2 * k + g], pair_recv.at[2 * k + g], chip_mate,
        )

    def gate_up_first():
        project(0, 0, (0, 1))

    def gate_up_second():
        for i in range(2):
            w_copies[i].wait_recv()
        project(0, 1, (0, 1))
        hand_over(0, 0)

    def gate_up_third():
        for copy in passed[0]:
            copy.wait_recv()
        project(1, 0, (0, 1))

    def gate_up_fourth():
        send_pair(0, 0)
        project(1, 1, (0, 1))
        hand_over(1, 0)

    near, far = list(range(GROUP)), list(range(GROUP, devices_ep))[::-1]
    arrivals = [(0, j) for j in near]
    for n, j in enumerate(far):
        arrivals.append((0, j))
        if 0 < n <= GROUP:
            arrivals.append((1, near[n - 1]))
    arrivals += [(1, j) for j in near if (1, j) not in arrivals]
    for n, j in arrivals:
        pass_on(n, j)
    for copy in own_w:
        copy.wait()
    gate_up_first()
    steps = [gate_up_second, gate_up_third, gate_up_fourth]
    for n, j in enumerate(far):
        pass_on(1, j)
        if n < len(steps):
            steps[n]()
    send_pair(1, 0)
    w_copies[2].wait_recv()
    for which in range(2):
        project(0, which, (2,))
    hand_over(0, 1)
    for copy in passed[1]:
        copy.wait_recv()
    for which in range(2):
        project(1, which, (2,))
    hand_over(1, 1)
    for k in range(2):
        send_pair(k, 1)
    for k in range(2):
        for g in range(2):
            pair_copies[k, g].wait_recv()

        def activate(at, k=k):
            total = [wide(pair[k, i, at, :]) + wide(across[k, i, at, :]) for i in range(3)]
            made = activations(*total)
            for i in range(3):
                act[k, core, at, i * hidden : (i + 1) * hidden] = made[i]

        by_rows(activate)
        act_copies.append(
            remote(
                act.at[k, core], act.at[k, core], act_send.at[k], act_recv.at[k], core_mate
            )
        )

    def transpose(which):
        for k in range(2):
            act_t[which, :, k * rows : (k + 1) * rows] = act[k, which].T

    for k in range(2):
        act_copies[k].wait_recv()
    transpose(1)

    def by_columns(fn):
        def one(n, carry):
            fn(pl.ds(pl.multiple_of(n * LANES, LANES), LANES))
            return carry

        lax.fori_loop(0, quarter // LANES, one, 0)

    def term(which, i, at):
        a = (i + 1) % 3 * hidden
        block = (x_all if i < 2 else d_all)[:, :, :, at].reshape(2 * rows, LANES)
        return jnp.dot(
            act_t[which, a : a + hidden, :], block, preferred_element_type=jnp.float32
        )

    def expert_dx(k, at):
        return sum(
            jnp.dot(
                act[k, which, :, (i + 1) * hidden : (i + 2) * hidden],
                w_all[which, i, :, at],
                preferred_element_type=jnp.float32,
            )
            for which in range(2)
            for i in range(2)
        ).reshape(devices_ep, capacity, LANES)

    term_copies = []
    for i in range(3):

        def make_term(at, i=i):
            term_out[i, :, at] = term(1, i, at).astype(jnp.bfloat16)

        by_columns(make_term)
        term_copies.append(
            remote(
                term_out.at[i], term_in.at[i], term_send.at[i], term_recv.at[i], weight_mate
            )
        )
        if i == 0:

            def make_dx(at):
                dx_out[:, :, at] = expert_dx(1, at).astype(jnp.bfloat16)

            by_columns(make_dx)
            dx_copies = {}
            for j in order + [0]:
                block = mate(j)
                dx_copies[j] = remote(
                    dx_out.at[block], dx_in.at[block], dx_send.at[j], dx_recv.at[j], row_mate
                )

    def own_dx(at):
        dx_own[:, :, at] = expert_dx(0, at)

    by_columns(own_dx)
    transpose(0)
    for i in range(3):

        def own_term(at, i=i):
            term_own[i, :, at] = term(0, i, at)

        by_columns(own_term)
    backs = []
    for j in order + [0]:
        block = mate(j)
        dx_copies[j].wait_recv()
        dx_sum[block] = (dx_own[block] + wide(dx_in[block])).astype(jnp.bfloat16)
        if j:
            backs.append(
                remote(
                    dx_sum.at[block], owned(slot_rows, s), back_send.at[j], back_recv.at[j],
                    (r, block),
                )
            )
        else:
            last = local(dx_sum.at[block], owned(slot_rows, s), self_sem.at[2])
    def take_back():
        last.wait()
        for copy in backs:
            copy.wait_recv()

        def fill_in(at):
            in_grad[:, at] = jnp.dot(
                pick_t[...], slot_rows[:, at], preferred_element_type=jnp.float32
            ).astype(jnp.bfloat16)

        by_slots(fill_in)

    for i, out in enumerate((grad_gate, grad_up, grad_down)):
        if i == 2:
            take_back()
        term_copies[i].wait_recv()

        def finish(at, i=i, out=out):
            out[:, at] = (term_own[i, :, at] + wide(term_in[i, :, at])).astype(jnp.bfloat16)

        by_columns(finish)
    sent = w_copies + list(x_copies.values()) + list(d_copies.values()) + passed[0] + passed[1]
    sent += list(give_copies.values()) + list(pair_copies.values()) + act_copies + term_copies + list(dx_copies.values())
    for copy in sent + backs:
        copy.wait_send()


def fast_body(tokens, out_grad, route_weight, expert_ids, w_gate, w_up, w_down):
    devices_ep = lax.axis_size("ep")
    experts = devices_ep // GROUP
    token_count = tokens.shape[0]
    capacity = 6 * GROUP * token_count * TOP // (8 * devices_ep)
    quarter = D // GROUP
    hidden = w_gate.shape[0]
    rows = devices_ep * capacity
    short = jnp.bfloat16
    _, _, token_of_slot, filled, weight_of_slot = slot_tables(
        expert_ids, route_weight, experts, capacity
    )
    token_ids = jnp.arange(token_count, dtype=jnp.int32)
    pick = ((token_of_slot[:, None] == token_ids[None, :]) & filled[:, None]).astype(short)
    pick_t = ((token_of_slot[None, :] == token_ids[:, None]) & filled[None, :]).astype(short)
    vmem = pl.BlockSpec(memory_space=pltpu.VMEM)
    hbm = pl.BlockSpec(memory_space=pl.ANY)
    grad = jax.ShapeDtypeStruct(w_gate.shape, short)
    dma = pltpu.SemaphoreType.DMA
    in_grad, grad_gate, grad_up, grad_down = pl.pallas_call(
        expert_kernel,
        out_shape=(jax.ShapeDtypeStruct(tokens.shape, short), grad, grad, grad),
        in_specs=[vmem, vmem, vmem, vmem, vmem, hbm, hbm, hbm],
        out_specs=(vmem, vmem, vmem, vmem),
        scratch_shapes=[
            pltpu.VMEM((experts * capacity, D), short),
            pltpu.VMEM((experts * capacity, D), short),
            pltpu.VMEM((experts * capacity, D), short),
            pltpu.VMEM((2, devices_ep, capacity, quarter), short),
            pltpu.VMEM((2, devices_ep, capacity, quarter), short),
            pltpu.VMEM((2, 3, hidden, quarter), short),
            pltpu.VMEM((2, 2, 3, rows, hidden), short),
            pltpu.VMEM((2, 3, rows, hidden), short),
            pltpu.VMEM((2, 3, rows, hidden), short),
            pltpu.VMEM((2, 3, rows, hidden), short),
            pltpu.VMEM((2, 2, rows, 3 * hidden), short),
            pltpu.VMEM((2, 3 * hidden, 2 * rows), short),
            pltpu.VMEM((3, hidden, quarter), short),
            pltpu.VMEM((3, hidden, quarter), short),
            pltpu.VMEM((3, hidden, quarter), jnp.float32),
            pltpu.VMEM((devices_ep, capacity, quarter), short),
            pltpu.VMEM((devices_ep, capacity, quarter), short),
            pltpu.VMEM((devices_ep, capacity, quarter), jnp.float32),
            pltpu.VMEM((devices_ep, capacity, quarter), short),
        ]
        + [dma((3,))] * 4
        + [dma((devices_ep,))] * 8
        + [dma((4,))] * 4
        + [dma((2,))] * 2
        + [dma((3,))] * 2
        + [dma((devices_ep,))] * 4,
        compiler_params=pltpu.CompilerParams(
            collective_id=0, has_side_effects=True, vmem_limit_bytes=60 * 2**20
        ),
    )(tokens, out_grad, pick, pick_t, weight_of_slot[:, None], w_gate, w_up, w_down)
    return (in_grad, grad_gate, grad_up, grad_down)


def solution(mesh):
    devices_ep = mesh.shape["ep"]

    def step(*arrays):
        capacity = 6 * GROUP * arrays[0].shape[0] * TOP // (8 * devices_ep)
        hidden = arrays[4].shape[0]
        fits = capacity % 48 == 0 and hidden % 128 == 0 and mesh.shape["dp"] == 4
        return (fast_body if fits else body)(*arrays)

    placed = (
        P(("dp", "ep"), None),
        P(("dp", "ep"), None),
        P(("dp", "ep"), None),
        P(("dp", "ep"), None),
        P("dp", "ep"),
        P("dp", "ep"),
        P("dp", "ep"),
    )
    return jax.shard_map(
        step,
        mesh=mesh,
        in_specs=placed,
        out_specs=(P(("dp", "ep"), None), P("dp", "ep"), P("dp", "ep"), P("dp", "ep")),
        check_vma=False,
    )
```

profile of v0, /device:TPU:0, one launch (start us, length us, event | category | flops | bytes accessed | tf_op | source)
XLA Modules:
  0.0 176.8 jit_solution(17567336184879362536)
XLA Ops:
  0.6 0.7 fusion
  1.4 0.2 reduce_window_sum.11
  1.5 0.8 select_reduce_fusion
  2.4 0.7 add_select_fusion
  3.1 0.1 fusion.4
  3.2 0.1 select_reduce_fusion.2
  3.3 0.8 select_reduce_fusion.1
  4.1 0.7 fusion.6.pick
  4.8 0.6 fusion.2.pick_t
  5.4 0.7 copy.12.scale
  6.1 164.4 %shard_map.102 = (bf16[128,7168]{1,0:T(8,128)(2,1)}, bf16[256,1792]{1,0:T(8,128)(2,1)}, bf16[256,1792]{1,0:T(8,128)(2,1)}, bf16[256,1792]{1,0:T(8,128)(2,1)}) custom-call(bf16[128,7168]{1,0:T(8,128)(2,1)} %tokens.1, bf16[128,7168]{1,0:T(8,128)(2,1)} %out_grad.1, bf16[96,128]{1,0:T(8,128)(2,1)} %fusion.6.pick, bf16[128,96]{1,0:T(8,128)(2,1)} %fusion.2.pick_t, ...), custom_call_target="tpu_custom_call" | custom-call | tf_op jit(solution)/shard_map/pallas_call | solution.py:515
  170.5 0.0 copy-start.2
  170.5 2.9 %copy.17 = bf16[128,7168]{1,0:T(8,128)(2,1)} copy(bf16[128,7168]{1,0:T(8,128)(2,1)} %get-tuple-element.8) | data formatting | bytes 3670016
  173.4 0.0 copy-done.2
  173.4 0.0 copy-start.1
  173.4 0.0 copy-start
  173.5 0.9 copy.18
  174.4 0.6 copy-done.1
  175.0 0.9 copy.19
  175.9 0.0 copy-done
  175.9 0.9 copy.20
  (1 shorter events, 0.0 us)
Async XLA Ops:
  170.5 2.9 %copy-start.2 = (bf16[256,1792]{1,0:T(8,128)(2,1)S(1)}, bf16[256,1792]{1,0:T(8,128)(2,1)}, u32[]{:S(2)}) copy-start(bf16[256,1792]{1,0:T(8,128)(2,1)} %get-tuple-element.9) | copy-start | bytes 2752516
  173.4 1.5 copy-start.1
  173.4 2.4 %copy-start = (bf16[256,1792]{1,0:T(8,128)(2,1)S(1)}, bf16[256,1792]{1,0:T(8,128)(2,1)}, u32[]{:S(2)}) copy-start(bf16[256,1792]{1,0:T(8,128)(2,1)} %get-tuple-element.11) | copy-start | bytes 2752516
where the time goes:
time: 178 us; the launch traced here: 177 us
  Pallas kernels  164 us (92%)
  local copies, waits for them, and re-layouts  7.01 us (4%)
  other arithmetic  4.75 us (3%)
    pallas_call x1, Pallas kernels, fast_body(): pl.pallas_call(expert_kernel, out_shape=(jax.ShapeDtypeStruct(tokens.shap...  164 us
    unnamed x10, local copies, waits for them, and re-layouts  6.29 us

commit v1 on v0

v1 whole, which is shorter than its diff:
```python
import jax
import jax.numpy as jnp
from jax import lax
from jax.experimental import pallas as pl
from jax.experimental.pallas import tpu as pltpu
from jax.sharding import PartitionSpec as P

D = 7168
GROUP = 4
TOP = 1


CONTRACT_LAST = (((1,), (1,)), ((), ()))
CONTRACT_FIRST = (((0,), (0,)), ((), ()))


def as_sent(value):

    def short(part):
        return part.astype(jnp.bfloat16) if part.dtype == jnp.float32 else part

    return jax.tree.map(short, value)


def from_partner(value, axis, distance):
    mask = 2**distance
    pairs = [(source, source ^ mask) for source in range(lax.axis_size(axis))]
    return lax.ppermute(value, axis, pairs)


def slot_tables(expert_ids, route_weight, experts, capacity):
    token_count, top_count = expert_ids.shape
    pair_count = token_count * top_count
    flat_ids = expert_ids.reshape(pair_count)
    onehot = (flat_ids[:, None] == jnp.arange(experts, dtype=jnp.int32)[None, :]).astype(jnp.int32)
    before = jnp.cumsum(onehot, axis=0) - onehot
    ranks = jnp.sum(before * onehot, axis=1)
    kept = ranks < capacity
    slots = jnp.where(kept, flat_ids * capacity + ranks, 0)
    slot_ids = jnp.arange(experts * capacity, dtype=jnp.int32)
    match = (slots[None, :] == slot_ids[:, None]) & kept[None, :]
    pair_ids = jnp.arange(pair_count, dtype=jnp.int32)
    pair_of_slot = jnp.sum(jnp.where(match, pair_ids[None, :], 0), axis=1)
    filled = jnp.any(match, axis=1)
    flat_weight = route_weight.reshape(pair_count)
    weight_of_slot = jnp.sum(jnp.where(match, flat_weight[None, :], jnp.float32(0.0)), axis=1)
    return (kept, slots, pair_of_slot // top_count, filled, weight_of_slot)


def activations(gate, up, back):
    logistic = jax.nn.sigmoid(gate)
    silu = gate * logistic
    hidden = (silu * up).astype(jnp.bfloat16)
    d_gate = (back * up * logistic * (1.0 + gate * (1.0 - logistic))).astype(jnp.bfloat16)
    d_up = (back * silu).astype(jnp.bfloat16)
    return (hidden, d_gate, d_up)


def swap(value, axis, distance):
    return from_partner(value, axis, distance)


def wide(value):
    return value.astype(jnp.float32)


def dot_last(left, right):
    return lax.dot_general(left, right, CONTRACT_LAST, preferred_element_type=jnp.float32)


def dot_first(left, right):
    return lax.dot_general(left, right, CONTRACT_FIRST, preferred_element_type=jnp.float32)


def body(tokens, out_grad, route_weight, expert_ids, w_gate, w_up, w_down):
    devices_ep = lax.axis_size("ep")
    experts = devices_ep // GROUP
    token_count = tokens.shape[0]
    capacity = 6 * GROUP * token_count * TOP // (8 * devices_ep)
    quarter = D // GROUP
    short = jnp.bfloat16
    kept, slots, token_of_slot, filled, weight_of_slot = slot_tables(
        expert_ids, route_weight, experts, capacity
    )
    other_w = tuple(swap(w, "dp", 1) for w in (w_gate, w_up, w_down))
    token_ids = jnp.arange(token_count, dtype=jnp.int32)
    pick = ((token_of_slot[:, None] == token_ids[None, :]) & filled[:, None]).astype(short)
    x_slots = jnp.dot(pick, tokens, preferred_element_type=jnp.float32).astype(short)
    d_slots = (
        jnp.dot(pick, out_grad, preferred_element_type=jnp.float32) * weight_of_slot[:, None]
    ).astype(short)

    def to_owners(rows):
        shaped = rows.reshape(experts, capacity, GROUP, quarter).transpose(0, 2, 1, 3)
        return shaped.reshape(devices_ep, capacity, quarter)

    def sent(rows):
        return lax.all_to_all(to_owners(rows), "ep", split_axis=0, concat_axis=0, tiled=True)

    row_count = devices_ep * capacity
    x_own = sent(x_slots).reshape(row_count, quarter)
    d_own = sent(d_slots).reshape(row_count, quarter)
    x_other, d_other = swap(x_own, "dp", 0), swap(d_own, "dp", 0)
    core = lax.axis_index("ep") % 2
    weights = ((w_gate, w_up, w_down), other_w)
    acts = []
    for x_rows, d_rows in ((x_own, d_own), (x_other, d_other)):
        terms = [
            jnp.concatenate(
                [dot_last(x_rows, wg), dot_last(x_rows, wu), dot_last(d_rows, wd)], axis=1
            ).astype(short)
            for wg, wu, wd in weights
        ]
        give = jnp.where(core == 0, terms[1], terms[0])
        keep = jnp.where(core == 0, terms[0], terms[1])
        pair = (wide(keep) + wide(swap(give, "ep", 0))).astype(short)
        total = wide(pair) + wide(swap(pair, "ep", 1))
        width = total.shape[1] // 3
        mine = jnp.concatenate(
            activations(total[:, :width], total[:, width : 2 * width], total[:, 2 * width :]), axis=1
        )
        theirs = swap(mine, "ep", 0)
        first = jnp.where(core == 0, mine, theirs)
        second = jnp.where(core == 0, theirs, mine)
        acts.append(
            tuple(
                tuple(half[:, piece * width : (piece + 1) * width] for piece in range(3))
                for half in (first, second)
            )
        )

    def grads(half):
        (h0, g0, u0), (h1, g1, u1) = acts[0][half], acts[1][half]
        return (
            dot_first(g0, x_own) + dot_first(g1, x_other),
            dot_first(u0, x_own) + dot_first(u1, x_other),
            dot_first(h0, d_own) + dot_first(h1, d_other),
        )

    def dx(rows):
        return sum(
            jnp.dot(acts[rows][half][1], weights[half][0], preferred_element_type=jnp.float32)
            + jnp.dot(acts[rows][half][2], weights[half][1], preferred_element_type=jnp.float32)
            for half in range(2)
        )

    dx_in = swap(dx(1).astype(short), "dp", 0)
    away = tuple(swap(term.astype(short), "dp", 1) for term in grads(1))
    expert_dx = (dx(0) + wide(dx_in)).astype(short)
    grad_gate, grad_up, grad_down = (
        (own + wide(term)).astype(short) for own, term in zip(grads(0), away)
    )
    returned = lax.all_to_all(
        expert_dx.reshape(devices_ep, capacity, quarter),
        "ep",
        split_axis=0,
        concat_axis=0,
        tiled=True,
    )
    slot_rows = (
        returned.reshape(experts, GROUP, capacity, quarter)
        .transpose(0, 2, 1, 3)
        .reshape(experts * capacity, D)
    )
    in_grad = dot_first(pick, slot_rows).astype(short)
    return (in_grad, grad_gate, grad_up, grad_down)

MESH = pl.DeviceIdType.MESH


def flip(index, bit):
    size = 1 << bit
    return index + size - 2 * size * lax.rem(lax.div(index, size), 2)


def expert_kernel(
    tokens, out_grad, route, ids, wg, wu, wd, in_grad, grad_gate, grad_up, grad_down,
    tok, ogr, pick, pick_t, scale, xs, ds, slot_rows, x_all, d_all, w_all, part, got, pair, across,
    act, act_t, term_out, term_in, term_own, dx_out, dx_in, dx_own, dx_sum,
    in_sem, w_local, w_send, w_recv, self_sem, x_send, x_recv, d_send, d_recv,
    fx_send, fx_recv, fd_send, fd_recv, give_send, give_recv, pair_send, pair_recv,
    act_send, act_recv, term_send, term_recv, dx_send, dx_recv, back_send, back_recv,
):
    devices_ep, capacity, quarter = dx_sum.shape
    rows = devices_ep * capacity
    half_rows = rows // 2
    hidden = wg.shape[0]
    slots, token_count = pick.shape
    experts = slots // capacity
    short = jnp.bfloat16
    r, s = lax.axis_index("dp"), lax.axis_index("ep")
    core, z = lax.rem(s, 2), lax.div(s, 2)
    side = lax.div(z, 2)
    at_end = lax.rem(z, 2) == side
    row_mate, weight_mate = (flip(r, 0), s), (flip(r, 1), s)
    core_mate, chip_mate = (r, flip(s, 0)), (r, flip(s, 1))
    far_mid, far_end = 2 * (2 - side), 2 * (3 - 3 * side)
    near = [flip(s, 1), flip(flip(s, 1), 0)]
    mids = [far_mid + core, far_mid + 1 - core]
    ends = [far_end + core, far_end + 1 - core]
    others = [flip(s, 0)] + near + ends + mids
    CORE, NEAR, FAR = [0], [1, 2], [3, 4, 5, 6]

    def local(source, target, sem):
        copy = pltpu.make_async_copy(source, target, sem)
        copy.start()
        return copy

    weights = (wg, wu, wd)
    own_w = [local(w, w_all.at[0, i], w_local.at[i]) for i, w in enumerate(weights)]
    tok_copy = local(tokens, tok, in_sem.at[0])
    ogr_copy = local(out_grad, ogr, in_sem.at[1])

    barrier = pltpu.get_barrier_semaphore()
    peers = [row_mate, weight_mate] + [(r, other) for other in others]
    for peer in peers:
        pl.semaphore_signal(barrier, inc=1, device_id=peer, device_id_type=MESH)

    named = ids[...]
    wide_rows = max(8, experts)
    expert_row = lax.broadcasted_iota(jnp.int32, (wide_rows, token_count), 0)
    onehot = jnp.where(expert_row == named, 1.0, 0.0)
    earlier = lax.broadcasted_iota(jnp.int32, (token_count, token_count), 0) < (
        lax.broadcasted_iota(jnp.int32, (token_count, token_count), 1)
    )
    before = jnp.dot(
        onehot.astype(short), jnp.where(earlier, 1.0, 0.0).astype(short),
        preferred_element_type=jnp.float32,
    )
    rank = jnp.sum(before * onehot, axis=0, keepdims=True)
    slot = jnp.where(rank < capacity, named.astype(jnp.float32) * capacity + rank, -1.0)
    slot_row = lax.broadcasted_iota(jnp.int32, (slots, token_count), 0).astype(jnp.float32)
    match = jnp.where(slot_row == slot, 1.0, 0.0)
    pick[...] = match.astype(short)
    scale[...] = jnp.sum(match * route[...], axis=1, keepdims=True)
    pick_t[...] = match.T.astype(short)

    pl.semaphore_wait(barrier, len(peers))

    def remote(source, target, send, recv, peer, start=True):
        copy = pltpu.make_async_remote_copy(
            src_ref=source, dst_ref=target, send_sem=send, recv_sem=recv,
            device_id=peer, device_id_type=MESH,
        )
        if start:
            copy.start()
        return copy

    def owned(ref, device):
        row = pl.multiple_of(lax.div(device, GROUP) * capacity, capacity)
        column = pl.multiple_of(lax.rem(device, GROUP) * quarter, 128)
        return ref.at[pl.ds(row, capacity), pl.ds(column, quarter)]

    w_copies = []
    for i in range(3):
        own_w[i].wait()
        w_copies.append(
            remote(w_all.at[0, i], w_all.at[1, i], w_send.at[i], w_recv.at[i], weight_mate)
        )

    def by_quarters(fn):
        def one(n, carry):
            fn(pl.ds(pl.multiple_of(n * quarter, quarter), quarter))
            return carry

        lax.fori_loop(0, GROUP, one, 0)

    def fill_x(at):
        xs[:, at] = jnp.dot(
            pick[...], tok[:, at], preferred_element_type=jnp.float32
        ).astype(short)

    def fill_d(at):
        ds[:, at] = (
            jnp.dot(pick[...], ogr[:, at], preferred_element_type=jnp.float32) * scale[...]
        ).astype(short)

    kinds = ((xs, x_all, x_send, x_recv), (ds, d_all, d_send, d_recv))

    def flow(kind, n):
        source, target, send, recv = kinds[kind]
        peer = others[n]
        return remote(
            owned(source, peer), target.at[0, s], send.at[n], recv.at[s], (r, peer), start=False
        )

    def send(kind, which):
        for n in which:
            flow(kind, n).start()

    self_copies = []
    tok_copy.wait()
    by_quarters(fill_x)
    send(0, CORE + NEAR)
    self_copies.append(local(owned(xs, s), x_all.at[0, s], self_sem.at[0]))

    @pl.when(jnp.logical_not(at_end))
    def _():
        send(0, FAR)

    ogr_copy.wait()
    by_quarters(fill_d)
    send(1, CORE + NEAR)
    self_copies.append(local(owned(ds, s), d_all.at[0, s], self_sem.at[1]))

    @pl.when(at_end)
    def _():
        send(0, FAR)

    passed = ([], [])

    def pass_on(kind, n):
        _, target, _, recv = kinds[kind]
        if n is None:
            origin = s
            self_copies[kind].wait()
        else:
            origin = others[n]
            remote(
                target.at[0, origin], target.at[0, origin], x_send.at[0], recv.at[origin],
                (r, origin), start=False,
            ).wait_recv()
        to_send, to_recv = ((fx_send, fx_recv), (fd_send, fd_recv))[kind]
        passed[kind].append(
            remote(
                target.at[0, origin], target.at[1, origin], to_send.at[origin],
                to_recv.at[origin], row_mate,
            )
        )

    def project(k, which, i):
        block = (x_all if i < 2 else d_all)[k].reshape(rows, quarter)
        part[k, which, i] = dot_last(block, w_all[which, i]).astype(short)

    STEP = 48

    def by_rows(fn):
        def one(n, carry):
            fn(pl.ds(pl.multiple_of(n * STEP, STEP), STEP))
            return carry

        lax.fori_loop(0, rows // STEP, one, 0)

    give_copies, pair_copies, act_copies = {}, {}, {}

    def hand_over(k, i):
        give_copies[k, i] = remote(
            part.at[k, 1 - core, i], got.at[k, i],
            give_send.at[3 * k + i], give_recv.at[3 * k + i], core_mate,
        )

    def send_pair(k, i):
        give_copies[k, i].wait_recv()

        def add_pair(at):
            pair[k, i, at, :] = (wide(part[k, core, i, at, :]) + wide(got[k, i, at, :])).astype(
                short
            )

        by_rows(add_pair)
        pair_copies[k, i] = remote(
            pair.at[k, i], across.at[k, i],
            pair_send.at[3 * k + i], pair_recv.at[3 * k + i], chip_mate,
        )

    def total(k, i, at):
        return wide(pair[k, i, at, :]) + wide(across[k, i, at, :])

    def make_hidden(k):
        for i in range(2):
            pair_copies[k, i].wait_recv()

        def one(at):
            gate, up = total(k, 0, at), total(k, 1, at)
            act[k, core, 0, at, :] = (gate * jax.nn.sigmoid(gate) * up).astype(short)

        by_rows(one)
        act_copies[k, 0] = remote(
            act.at[k, core, 0], act.at[k, core, 0],
            act_send.at[2 * k], act_recv.at[2 * k], core_mate,
        )

    def make_slopes(k):
        pair_copies[k, 2].wait_recv()

        def one(at):
            made = activations(total(k, 0, at), total(k, 1, at), total(k, 2, at))
            act[k, core, 1, at, :] = made[1]
            act[k, core, 2, at, :] = made[2]

        by_rows(one)
        act_copies[k, 1] = remote(
            act.at[k, core, pl.ds(1, 2)], act.at[k, core, pl.ds(1, 2)],
            act_send.at[2 * k + 1], act_recv.at[2 * k + 1], core_mate,
        )

    def transpose(which, piece):
        for k in range(2):
            act_t[which, piece, :, k * rows : (k + 1) * rows] = act[k, which, piece].T

    LANES = 896

    def by_columns(fn):
        def one(n, carry):
            fn(pl.ds(pl.multiple_of(n * LANES, LANES), LANES))
            return carry

        lax.fori_loop(0, quarter // LANES, one, 0)

    def term(which, i, at):
        block = (x_all if i < 2 else d_all)[:, :, :, at].reshape(2 * rows, LANES)
        return jnp.dot(
            act_t[which, (i + 1) % 3], block, preferred_element_type=jnp.float32
        )

    CUTS = 4
    term_copies = {}

    def send_term(i):
        def make(at):
            term_out[i, :, at] = term(1, i, at).astype(short)

        by_columns(make)
        size = hidden // CUTS
        for n in range(CUTS):
            cut = pl.ds(n * size, size)
            term_copies[i, n] = remote(
                term_out.at[i, cut], term_in.at[i, cut],
                term_send.at[CUTS * i + n], term_recv.at[CUTS * i + n], weight_mate,
            )

    def own_term(i):
        def make(at):
            term_own[i, :, at] = term(0, i, at)

        by_columns(make)

    def finish(i):
        size = hidden // CUTS
        out = (grad_gate, grad_up, grad_down)[i]
        for n in range(CUTS):
            cut = pl.ds(n * size, size)
            term_copies[i, n].wait_recv()
            out[cut, :] = (term_own[i, cut, :] + wide(term_in[i, cut, :])).astype(short)

    def expert_dx(k, part_of, at):
        here = pl.ds(pl.multiple_of(part_of * half_rows, half_rows), half_rows)
        return sum(
            jnp.dot(
                act[k, which, i + 1, here, :], w_all[which, i, :, at],
                preferred_element_type=jnp.float32,
            )
            for which in range(2)
            for i in range(2)
        ).reshape(devices_ep // 2, capacity, LANES)

    dx_blocks = ends + mids + near + [flip(s, 0), s]
    dx_copies = []

    def send_dx(part_of, blocks):
        here = pl.ds(part_of * (devices_ep // 2), devices_ep // 2)

        def make(at):
            dx_out[here, :, at] = expert_dx(1, part_of, at).astype(short)

        by_columns(make)
        for n in blocks:
            block = dx_blocks[n]
            dx_copies.append(
                remote(
                    dx_out.at[block], dx_in.at[block], dx_send.at[n], dx_recv.at[n], row_mate
                )
            )

    def own_dx(part_of):
        here = pl.ds(part_of * (devices_ep // 2), devices_ep // 2)

        def make(at):
            dx_own[here, :, at] = expert_dx(0, part_of, at)

        by_columns(make)

    backs = []

    def give_back(n):
        block = dx_blocks[n]
        dx_copies[n].wait_recv()
        dx_sum[block] = (dx_own[block] + wide(dx_in[block])).astype(short)
        if n < devices_ep - 1:
            backs.append(
                remote(
                    dx_sum.at[block], owned(slot_rows, s), back_send.at[n], back_recv.at[s],
                    (r, block),
                )
            )
        else:
            backs.append(local(dx_sum.at[block], owned(slot_rows, s), self_sem.at[2]))

    pass_on(0, None)
    for n in CORE + NEAR:
        pass_on(0, n)
    pass_on(0, 5)
    pass_on(0, 6)
    pass_on(1, None)
    pass_on(0, 3)
    pass_on(0, 4)

    @pl.when(jnp.logical_not(at_end))
    def _():
        send(1, FAR)

    @pl.when(at_end)
    def _():
        send(1, FAR[:1])

    for n in CORE + NEAR:
        pass_on(1, n)
    project(0, 0, 0)
    w_copies[0].wait_recv()
    project(0, 1, 0)
    hand_over(0, 0)
    project(0, 0, 1)
    send_pair(0, 0)
    for copy in passed[0]:
        copy.wait_recv()
    project(1, 0, 0)
    project(1, 1, 0)
    hand_over(1, 0)
    project(1, 0, 1)
    send_pair(1, 0)

    @pl.when(at_end)
    def _():
        send(1, FAR[1:])

    pass_on(1, 5)
    w_copies[1].wait_recv()
    project(0, 1, 1)
    hand_over(0, 1)
    project(1, 1, 1)
    hand_over(1, 1)
    pass_on(1, 6)
    send_pair(0, 1)
    send_pair(1, 1)
    pass_on(1, 3)
    pass_on(1, 4)
    project(0, 0, 2)
    make_hidden(0)
    make_hidden(1)
    w_copies[2].wait_recv()
    project(0, 1, 2)
    hand_over(0, 2)
    for copy in passed[1]:
        copy.wait_recv()
    project(1, 0, 2)
    project(1, 1, 2)
    hand_over(1, 2)
    send_pair(0, 2)
    for k in range(2):
        act_copies[k, 0].wait_recv()
    transpose(1, 0)
    send_term(2)
    send_pair(1, 2)
    transpose(0, 0)
    own_term(2)
    make_slopes(0)
    make_slopes(1)
    act_copies[0, 1].wait_recv()
    act_copies[1, 1].wait_recv()
    send_dx(1 - side, range(0, 4))
    send_dx(side, range(4, 8))
    transpose(1, 1)
    send_term(0)
    transpose(1, 2)
    send_term(1)
    own_dx(1 - side)
    for n in range(4):
        give_back(n)
    own_dx(side)
    finish(2)
    transpose(0, 1)
    own_term(0)
    transpose(0, 2)
    own_term(1)
    for n in range(4, 8):
        give_back(n)
    finish(0)
    backs[-1].wait()
    for origin in others:
        remote(
            dx_sum.at[0], owned(slot_rows, origin), back_send.at[0], back_recv.at[origin],
            (r, origin), start=False,
        ).wait_recv()

    def fill_in(at):
        in_grad[:, at] = jnp.dot(
            pick_t[...], slot_rows[:, at], preferred_element_type=jnp.float32
        ).astype(short)

    by_quarters(fill_in)
    finish(1)
    for kind in range(2):
        for n in range(devices_ep - 1):
            flow(kind, n).wait_send()
    sent = w_copies + passed[0] + passed[1] + list(give_copies.values())
    sent += list(pair_copies.values()) + list(act_copies.values())
    sent += list(term_copies.values()) + dx_copies + backs[:-1]
    for copy in sent:
        copy.wait_send()


def fast_body(tokens, out_grad, route_weight, expert_ids, w_gate, w_up, w_down):
    devices_ep = lax.axis_size("ep")
    experts = devices_ep // GROUP
    token_count = tokens.shape[0]
    capacity = 6 * GROUP * token_count * TOP // (8 * devices_ep)
    quarter = D // GROUP
    hidden = w_gate.shape[0]
    rows = devices_ep * capacity
    slots = experts * capacity
    short = jnp.bfloat16
    vmem = pl.BlockSpec(memory_space=pltpu.VMEM)
    hbm = pl.BlockSpec(memory_space=pl.ANY)
    grad = jax.ShapeDtypeStruct(w_gate.shape, short)
    dma = pltpu.SemaphoreType.DMA
    in_grad, grad_gate, grad_up, grad_down = pl.pallas_call(
        expert_kernel,
        out_shape=(jax.ShapeDtypeStruct(tokens.shape, short), grad, grad, grad),
        in_specs=[hbm, hbm, vmem, vmem, hbm, hbm, hbm],
        out_specs=(vmem, vmem, vmem, vmem),
        scratch_shapes=[
            pltpu.VMEM(tokens.shape, short),
            pltpu.VMEM(tokens.shape, short),
            pltpu.VMEM((slots, token_count), short),
            pltpu.VMEM((token_count, slots), short),
            pltpu.VMEM((slots, 1), jnp.float32),
            pltpu.VMEM((slots, D), short),
            pltpu.VMEM((slots, D), short),
            pltpu.VMEM((slots, D), short),
            pltpu.VMEM((2, devices_ep, capacity, quarter), short),
            pltpu.VMEM((2, devices_ep, capacity, quarter), short),
            pltpu.VMEM((2, 3, hidden, quarter), short),
            pltpu.VMEM((2, 2, 3, rows, hidden), short),
            pltpu.VMEM((2, 3, rows, hidden), short),
            pltpu.VMEM((2, 3, rows, hidden), short),
            pltpu.VMEM((2, 3, rows, hidden), short),
            pltpu.VMEM((2, 2, 3, rows, hidden), short),
            pltpu.VMEM((2, 3, hidden, 2 * rows), short),
            pltpu.VMEM((3, hidden, quarter), short),
            pltpu.VMEM((3, hidden, quarter), short),
            pltpu.VMEM((3, hidden, quarter), jnp.float32),
            pltpu.VMEM((devices_ep, capacity, quarter), short),
            pltpu.VMEM((devices_ep, capacity, quarter), short),
            pltpu.VMEM((devices_ep, capacity, quarter), jnp.float32),
            pltpu.VMEM((devices_ep, capacity, quarter), short),
        ]
        + [dma((2,))]
        + [dma((3,))] * 4
        + [dma((devices_ep,))] * 8
        + [dma((6,))] * 4
        + [dma((4,))] * 2
        + [dma((12,))] * 2
        + [dma((devices_ep,))] * 4,
        compiler_params=pltpu.CompilerParams(
            collective_id=0, has_side_effects=True, vmem_limit_bytes=60 * 2**20
        ),
    )(
        tokens, out_grad, route_weight.reshape(1, token_count),
        expert_ids.reshape(1, token_count), w_gate, w_up, w_down,
    )
    return (in_grad, grad_gate, grad_up, grad_down)


def solution(mesh):
    devices_ep = mesh.shape["ep"]

    def step(*arrays):
        token_count = arrays[0].shape[0]
        capacity = 6 * GROUP * token_count * TOP // (8 * devices_ep)
        hidden = arrays[4].shape[0]
        fits = capacity % 48 == 0 and hidden % 128 == 0 and token_count % 128 == 0
        fits = fits and mesh.shape["dp"] == 4 and devices_ep == 2 * GROUP
        return (fast_body if fits else body)(*arrays)

    placed = (
        P(("dp", "ep"), None),
        P(("dp", "ep"), None),
        P(("dp", "ep"), None),
        P(("dp", "ep"), None),
        P("dp", "ep"),
        P("dp", "ep"),
        P("dp", "ep"),
    )
    return jax.shard_map(
        step,
        mesh=mesh,
        in_specs=placed,
        out_specs=(P(("dp", "ep"), None), P("dp", "ep"), P("dp", "ep"), P("dp", "ep")),
        check_vma=False,
    )
```

time: 178 us -> 155 us (0.87)
  Pallas kernels: 164 us -> 148 us
  other arithmetic: 4.75 us -> 0 us
    pallas_call x1, Pallas kernels: 164 us -> 148 us  [fast_body(): pl.pallas_call(expert_kernel, out_shape=(jax.ShapeDtypeStruct(tokens.shap...]
    convert_element_type x3 -> x0, other arithmetic: 2.08 us -> none  [the longest x1 0.74 us: slot_tables(): (flat_ids[:, None] == jnp.arange(experts, dtype=jnp.int32)[None, :]).asty...]
where the time goes in v1:
time: 155 us
  Pallas kernels  148 us (95%)
  local copies, waits for them, and re-layouts  6.29 us (4%)
    pallas_call x1, Pallas kernels, fast_body(): pl.pallas_call(expert_kernel, out_shape=(jax.ShapeDtypeStruct(tokens.shap...  148 us
    unnamed x10, local copies, waits for them, and re-layouts  6.29 us

profile of v1, /device:TPU:0, one launch (start us, length us, event | category | flops | bytes accessed | tf_op | source)
XLA Modules:
  0.0 154.5 jit_solution(5083686523185334934)
XLA Ops:
  0.6 147.6 %shard_map.102 = (bf16[128,7168]{1,0:T(8,128)(2,1)}, bf16[256,1792]{1,0:T(8,128)(2,1)}, bf16[256,1792]{1,0:T(8,128)(2,1)}, bf16[256,1792]{1,0:T(8,128)(2,1)}) custom-call(bf16[128,7168]{1,0:T(8,128)(2,1)} %tokens.1, bf16[128,7168]{1,0:T(8,128)(2,1)} %out_grad.1, f32[1,128]{1,0:T(1,128)} %bitcast.2, s32[1,128]{1,0:T(1,128)} %bitcast.3, bf16[256,1792]{1,0:T(8,128)(2,1)} %wg.1, ...), custom_call_target="tpu_custom_call" | custom-call | tf_op jit(solution)/shard_map/pallas_call | solution.py:626
  148.2 0.0 copy-start.2
  148.2 2.9 %copy.15 = bf16[128,7168]{1,0:T(8,128)(2,1)} copy(bf16[128,7168]{1,0:T(8,128)(2,1)} %get-tuple-element.8) | data formatting | bytes 3670016
  151.2 0.0 copy-done.2
  151.2 0.0 copy-start.1
  151.2 0.0 copy-start
  151.2 0.9 copy.16
  152.1 0.6 copy-done.1
  152.7 0.9 copy.17
  153.6 0.0 copy-done
  153.6 0.9 copy.18
Async XLA Ops:
  148.2 2.9 %copy-start.2 = (bf16[256,1792]{1,0:T(8,128)(2,1)S(1)}, bf16[256,1792]{1,0:T(8,128)(2,1)}, u32[]{:S(2)}) copy-start(bf16[256,1792]{1,0:T(8,128)(2,1)} %get-tuple-element.9) | copy-start | bytes 2752516
  151.2 1.5 copy-start.1
  151.2 2.4 %copy-start = (bf16[256,1792]{1,0:T(8,128)(2,1)S(1)}, bf16[256,1792]{1,0:T(8,128)(2,1)}, u32[]{:S(2)}) copy-start(bf16[256,1792]{1,0:T(8,128)(2,1)} %get-tuple-element.11) | copy-start | bytes 2752516

commit v2 on v1

--- a/solution.py
+++ b/solution.py
@@ -175,7 +175,7 @@
 
 def expert_kernel(
     tokens, out_grad, route, ids, wg, wu, wd, in_grad, grad_gate, grad_up, grad_down,
-    tok, ogr, pick, pick_t, scale, xs, ds, slot_rows, x_all, d_all, w_all, part, got, pair, across,
+    named, paid, tok, ogr, pick, pick_t, scale, xs, ds, slot_rows, x_all, d_all, w_all, part, got, pair, across,
     act, act_t, term_out, term_in, term_own, dx_out, dx_in, dx_own, dx_sum,
     in_sem, w_local, w_send, w_recv, self_sem, x_send, x_recv, d_send, d_recv,
     fx_send, fx_recv, fd_send, fd_recv, give_send, give_recv, pair_send, pair_recv,
@@ -191,7 +191,8 @@
     r, s = lax.axis_index("dp"), lax.axis_index("ep")
     core, z = lax.rem(s, 2), lax.div(s, 2)
     side = lax.div(z, 2)
-    at_end = lax.rem(z, 2) == side
+    end = 1 - lax.rem(z + side, 2)
+    at_end = end == 1
     row_mate, weight_mate = (flip(r, 0), s), (flip(r, 1), s)
     core_mate, chip_mate = (r, flip(s, 0)), (r, flip(s, 1))
     far_mid, far_end = 2 * (2 - side), 2 * (3 - 3 * side)
@@ -206,8 +207,9 @@
         copy.start()
         return copy
 
+    small = [local(ids, named, in_sem.at[2]), local(route, paid, in_sem.at[3])]
     weights = (wg, wu, wd)
-    own_w = [local(w, w_all.at[0, i], w_local.at[i]) for i, w in enumerate(weights)]
+    own_w = [local(w, w_all.at[i, 0], w_local.at[i]) for i, w in enumerate(weights)]
     tok_copy = local(tokens, tok, in_sem.at[0])
     ogr_copy = local(out_grad, ogr, in_sem.at[1])
 
@@ -216,10 +218,12 @@
     for peer in peers:
         pl.semaphore_signal(barrier, inc=1, device_id=peer, device_id_type=MESH)
 
-    named = ids[...]
+    for copy in small:
+        copy.wait()
+    name = named[...]
     wide_rows = max(8, experts)
     expert_row = lax.broadcasted_iota(jnp.int32, (wide_rows, token_count), 0)
-    onehot = jnp.where(expert_row == named, 1.0, 0.0)
+    onehot = jnp.where(expert_row == name, 1.0, 0.0)
     earlier = lax.broadcasted_iota(jnp.int32, (token_count, token_count), 0) < (
         lax.broadcasted_iota(jnp.int32, (token_count, token_count), 1)
     )
@@ -228,11 +232,11 @@
         preferred_element_type=jnp.float32,
     )
     rank = jnp.sum(before * onehot, axis=0, keepdims=True)
-    slot = jnp.where(rank < capacity, named.astype(jnp.float32) * capacity + rank, -1.0)
+    slot = jnp.where(rank < capacity, name.astype(jnp.float32) * capacity + rank, -1.0)
     slot_row = lax.broadcasted_iota(jnp.int32, (slots, token_count), 0).astype(jnp.float32)
     match = jnp.where(slot_row == slot, 1.0, 0.0)
     pick[...] = match.astype(short)
-    scale[...] = jnp.sum(match * route[...], axis=1, keepdims=True)
+    scale[...] = jnp.sum(match * paid[...], axis=1, keepdims=True)
     pick_t[...] = match.T.astype(short)
 
     pl.semaphore_wait(barrier, len(peers))
@@ -255,7 +259,7 @@
     for i in range(3):
         own_w[i].wait()
         w_copies.append(
-            remote(w_all.at[0, i], w_all.at[1, i], w_send.at[i], w_recv.at[i], weight_mate)
+            remote(w_all.at[i, 0], w_all.at[i, 1], w_send.at[i], w_recv.at[i], weight_mate)
         )
 
     def by_quarters(fn):
@@ -328,9 +332,11 @@
             )
         )
 
-    def project(k, which, i):
+    def project(k, i):
         block = (x_all if i < 2 else d_all)[k].reshape(rows, quarter)
-        part[k, which, i] = dot_last(block, w_all[which, i]).astype(short)
+        both = dot_last(block, w_all[i].reshape(2 * hidden, quarter)).astype(short)
+        for which in range(2):
+            part[k, which, i] = both[:, which * hidden : (which + 1) * hidden]
 
     STEP = 48
 
@@ -407,23 +413,23 @@
 
         lax.fori_loop(0, quarter // LANES, one, 0)
 
-    def term(which, i, at):
+    def term(which, i, cut, at):
         block = (x_all if i < 2 else d_all)[:, :, :, at].reshape(2 * rows, LANES)
         return jnp.dot(
-            act_t[which, (i + 1) % 3], block, preferred_element_type=jnp.float32
-        )
-
-    CUTS = 4
+            act_t[which, (i + 1) % 3, cut, :], block, preferred_element_type=jnp.float32
+        )
+
+    CUTS = 2
+    cuts = [pl.ds(n * (hidden // CUTS), hidden // CUTS) for n in range(CUTS)]
     term_copies = {}
 
     def send_term(i):
-        def make(at):
-            term_out[i, :, at] = term(1, i, at).astype(short)
-
-        by_columns(make)
-        size = hidden // CUTS
-        for n in range(CUTS):
-            cut = pl.ds(n * size, size)
+        for n, cut in enumerate(cuts):
+
+            def make(at, cut=cut):
+                term_out[i, cut, at] = term(1, i, cut, at).astype(short)
+
+            by_columns(make)
             term_copies[i, n] = remote(
                 term_out.at[i, cut], term_in.at[i, cut],
                 term_send.at[CUTS * i + n], term_recv.at[CUTS * i + n], weight_mate,
@@ -431,15 +437,13 @@
 
     def own_term(i):
         def make(at):
-            term_own[i, :, at] = term(0, i, at)
+            term_own[i, :, at] = term(0, i, slice(None), at)
 
         by_columns(make)
 
     def finish(i):
-        size = hidden // CUTS
         out = (grad_gate, grad_up, grad_down)[i]
-        for n in range(CUTS):
-            cut = pl.ds(n * size, size)
+        for n, cut in enumerate(cuts):
             term_copies[i, n].wait_recv()
             out[cut, :] = (term_own[i, cut, :] + wide(term_in[i, cut, :])).astype(short)
 
@@ -447,7 +451,7 @@
         here = pl.ds(pl.multiple_of(part_of * half_rows, half_rows), half_rows)
         return sum(
             jnp.dot(
-                act[k, which, i + 1, here, :], w_all[which, i, :, at],
+                act[k, which, i + 1, here, :], w_all[i, which, :, at],
                 preferred_element_type=jnp.float32,
             )
             for which in range(2)
@@ -496,72 +500,67 @@
         else:
             backs.append(local(dx_sum.at[block], owned(slot_rows, s), self_sem.at[2]))
 
-    pass_on(0, None)
-    for n in CORE + NEAR:
+    for kind in range(2):
+        pass_on(kind, None)
+        for n in CORE:
+            pass_on(kind, n)
+    for n in (1, 2, 5, 6, 3, 4):
         pass_on(0, n)
-    pass_on(0, 5)
-    pass_on(0, 6)
-    pass_on(1, None)
-    pass_on(0, 3)
-    pass_on(0, 4)
 
     @pl.when(jnp.logical_not(at_end))
     def _():
-        send(1, FAR)
+        send(1, (3, 4, 5, 6))
 
     @pl.when(at_end)
     def _():
-        send(1, FAR[:1])
-
-    for n in CORE + NEAR:
+        send(1, (3, 4))
+
+    for n in NEAR:
         pass_on(1, n)
-    project(0, 0, 0)
     w_copies[0].wait_recv()
-    project(0, 1, 0)
+    project(0, 0)
     hand_over(0, 0)
-    project(0, 0, 1)
     send_pair(0, 0)
+
+    @pl.when(at_end)
+    def _():
+        send(1, (5,))
+
     for copy in passed[0]:
         copy.wait_recv()
-    project(1, 0, 0)
-    project(1, 1, 0)
+    project(1, 0)
     hand_over(1, 0)
-    project(1, 0, 1)
+    w_copies[1].wait_recv()
+    project(0, 1)
+    hand_over(0, 1)
     send_pair(1, 0)
+    project(1, 1)
+    hand_over(1, 1)
+    send_pair(0, 1)
 
     @pl.when(at_end)
     def _():
-        send(1, FAR[1:])
-
-    pass_on(1, 5)
-    w_copies[1].wait_recv()
-    project(0, 1, 1)
-    hand_over(0, 1)
-    project(1, 1, 1)
-    hand_over(1, 1)
-    pass_on(1, 6)
-    send_pair(0, 1)
+        send(1, (6,))
+
     send_pair(1, 1)
-    pass_on(1, 3)
-    pass_on(1, 4)
-    project(0, 0, 2)
+    for n in (3, 5, 4, 6):
+        pass_on(1, n)
+    w_copies[2].wait_recv()
+    project(0, 2)
+    hand_over(0, 2)
     make_hidden(0)
     make_hidden(1)
-    w_copies[2].wait_recv()
-    project(0, 1, 2)
-    hand_over(0, 2)
-    for copy in passed[1]:
-        copy.wait_recv()
-    project(1, 0, 2)
-    project(1, 1, 2)
-    hand_over(1, 2)
     send_pair(0, 2)
     for k in range(2):
         act_copies[k, 0].wait_recv()
     transpose(1, 0)
+    for copy in passed[1]:
+        copy.wait_recv()
     send_term(2)
+    project(1, 2)
+    hand_over(1, 2)
+    transpose(0, 0)
     send_pair(1, 2)
-    transpose(0, 0)
     own_term(2)
     make_slopes(0)
     make_slopes(1)
@@ -609,6 +608,17 @@
         copy.wait_send()
 
 
+def store_kernel(*refs):
+    count = len(refs) // 2
+    copies = [
+        pltpu.make_async_copy(refs[i], refs[count + i], refs[-1].at[i]) for i in range(count)
+    ]
+    for copy in copies:
+        copy.start()
+    for copy in copies:
+        copy.wait()
+
+
 def fast_body(tokens, out_grad, route_weight, expert_ids, w_gate, w_up, w_down):
     devices_ep = lax.axis_size("ep")
     experts = devices_ep // GROUP
@@ -620,15 +630,17 @@
     slots = experts * capacity
     short = jnp.bfloat16
     vmem = pl.BlockSpec(memory_space=pltpu.VMEM)
-    hbm = pl.BlockSpec(memory_space=pl.ANY)
+    far = pl.BlockSpec(memory_space=pltpu.HBM)
     grad = jax.ShapeDtypeStruct(w_gate.shape, short)
     dma = pltpu.SemaphoreType.DMA
-    in_grad, grad_gate, grad_up, grad_down = pl.pallas_call(
+    results = pl.pallas_call(
         expert_kernel,
         out_shape=(jax.ShapeDtypeStruct(tokens.shape, short), grad, grad, grad),
-        in_specs=[hbm, hbm, vmem, vmem, hbm, hbm, hbm],
+        in_specs=[far] * 7,
         out_specs=(vmem, vmem, vmem, vmem),
         scratch_shapes=[
+            pltpu.VMEM((1, token_count), jnp.int32),
+            pltpu.VMEM((1, token_count), jnp.float32),
             pltpu.VMEM(tokens.shape, short),
             pltpu.VMEM(tokens.shape, short),
             pltpu.VMEM((slots, token_count), short),
@@ -639,7 +651,7 @@
             pltpu.VMEM((slots, D), short),
             pltpu.VMEM((2, devices_ep, capacity, quarter), short),
             pltpu.VMEM((2, devices_ep, capacity, quarter), short),
-            pltpu.VMEM((2, 3, hidden, quarter), short),
+            pltpu.VMEM((3, 2, hidden, quarter), short),
             pltpu.VMEM((2, 2, 3, rows, hidden), short),
             pltpu.VMEM((2, 3, rows, hidden), short),
             pltpu.VMEM((2, 3, rows, hidden), short),
@@ -654,21 +666,30 @@
             pltpu.VMEM((devices_ep, capacity, quarter), jnp.float32),
             pltpu.VMEM((devices_ep, capacity, quarter), short),
         ]
-        + [dma((2,))]
+        + [dma((4,))]
         + [dma((3,))] * 4
         + [dma((devices_ep,))] * 8
         + [dma((6,))] * 4
         + [dma((4,))] * 2
-        + [dma((12,))] * 2
+        + [dma((6,))] * 2
         + [dma((devices_ep,))] * 4,
         compiler_params=pltpu.CompilerParams(
-            collective_id=0, has_side_effects=True, vmem_limit_bytes=60 * 2**20
+            collective_id=0, has_side_effects=True, vmem_limit_bytes=52 * 2**20
         ),
     )(
         tokens, out_grad, route_weight.reshape(1, token_count),
         expert_ids.reshape(1, token_count), w_gate, w_up, w_down,
     )
-    return (in_grad, grad_gate, grad_up, grad_down)
+    return tuple(
+        pl.pallas_call(
+            store_kernel,
+            out_shape=tuple(jax.ShapeDtypeStruct(v.shape, v.dtype) for v in results),
+            in_specs=[vmem] * len(results),
+            out_specs=(far,) * len(results),
+            scratch_shapes=[dma((len(results),))],
+            compiler_params=pltpu.CompilerParams(vmem_limit_bytes=8 * 2**20),
+        )(*results)
+    )
 
 
 def solution(mesh):

time: 155 us -> 145 us (0.935)
  Pallas kernels: 148 us -> 139 us
  local copies, waits for them, and re-layouts: 6.29 us -> 3.97 us
    pallas_call x1, Pallas kernels: 148 us -> 137 us  [fast_body(): pl.pallas_call(expert_kernel, out_shape=(jax.ShapeDtypeStruct(tokens.shap...]
    unnamed x10 -> x8, local copies, waits for them, and re-layouts: 6.29 us -> 3.97 us
    pallas_call x0 -> x1, Pallas kernels: none -> 2.16 us  [fast_body(): pl.pallas_call(store_kernel, out_shape=tuple((jax.ShapeDtypeStruct(v.shap...]
where the time goes in v2:
time: 145 us; the launch traced here: 144 us
  Pallas kernels  139 us (96%)
  local copies, waits for them, and re-layouts  3.97 us (3%)
    pallas_call x1, Pallas kernels, fast_body(): pl.pallas_call(expert_kernel, out_shape=(jax.ShapeDtypeStruct(tokens.shap...  137 us
    unnamed x8, local copies, waits for them, and re-layouts  3.97 us

profile of v2, /device:TPU:0, one launch (start us, length us, event | category | flops | bytes accessed | tf_op | source)
XLA Modules:
  0.0 144.0 jit_solution(12347652233089248253)
XLA Ops:
  0.6 0.0 copy-start.2
  0.6 0.6 copy-done.2
  1.3 0.0 copy-start.3
  1.3 0.7 copy-done.3
  1.9 137.3 %shard_map.102 = (bf16[128,7168]{1,0:T(8,128)(2,1)}, bf16[256,1792]{1,0:T(8,128)(2,1)S(1)}, bf16[256,1792]{1,0:T(8,128)(2,1)S(1)}, bf16[256,1792]{1,0:T(8,128)(2,1)}) custom-call(bf16[128,7168]{1,0:T(8,128)(2,1)} %tokens.1, bf16[128,7168]{1,0:T(8,128)(2,1)} %out_grad.1, f32[1,128]{1,0:T(1,128)S(1)} %bitcast.2, s32[1,128]{1,0:T(1,128)S(1)} %bitcast.3, ...), custom_call_target="tpu_custom_call" | custom-call | tf_op jit(solution)/shard_map/pallas_call | solution.py:636
  139.2 0.0 copy-start
  139.2 1.5 %copy-done = bf16[128,7168]{1,0:T(8,128)(2,1)S(1)} copy-done((bf16[128,7168]{1,0:T(8,128)(2,1)S(1)}, bf16[128,7168]{1,0:T(8,128)(2,1)}, u32[]{:S(2)}) %copy-start) | copy-done | bytes 1835032
  140.7 0.0 copy-start.1
  140.7 1.2 copy-done.1
  141.9 2.2 %shard_map.103 = (bf16[128,7168]{1,0:T(8,128)(2,1)}, bf16[256,1792]{1,0:T(8,128)(2,1)}, bf16[256,1792]{1,0:T(8,128)(2,1)}, bf16[256,1792]{1,0:T(8,128)(2,1)}) custom-call(bf16[128,7168]{1,0:T(8,128)(2,1)S(1)} %copy-done, bf16[256,1792]{1,0:T(8,128)(2,1)S(1)} %get-tuple-element.9.refs_1_, bf16[256,1792]{1,0:T(8,128)(2,1)S(1)} %get-tuple-element.10.refs_2_, ...), custom_call_target="tpu_custom_call" | custom-call | tf_op jit(solution)/shard_map/pallas_call | solution.py:684
Async XLA Ops:
  0.6 0.7 copy-start.2
  1.3 0.7 copy-start.3
  139.2 1.5 %copy-start = (bf16[128,7168]{1,0:T(8,128)(2,1)S(1)}, bf16[128,7168]{1,0:T(8,128)(2,1)}, u32[]{:S(2)}) copy-start(bf16[128,7168]{1,0:T(8,128)(2,1)} %get-tuple-element.8.refs_0_) | copy-start | bytes 5505028
  140.7 1.2 copy-start.1

commit v3 on v2

--- a/solution.py
+++ b/solution.py
@@ -174,10 +174,10 @@
 
 
 def expert_kernel(
-    tokens, out_grad, route, ids, wg, wu, wd, in_grad, grad_gate, grad_up, grad_down,
+    tokens, out_grad, route, ids, wg, wu, wd, in_0, in_1, in_2, in_3, grad_gate, grad_up, grad_down,
     named, paid, tok, ogr, pick, pick_t, scale, xs, ds, slot_rows, x_all, d_all, w_all, part, got, pair, across,
     act, act_t, term_out, term_in, term_own, dx_out, dx_in, dx_own, dx_sum,
-    in_sem, w_local, w_send, w_recv, self_sem, x_send, x_recv, d_send, d_recv,
+    in_sem, tok_sem, w_local, w_send, w_recv, self_sem, x_send, x_recv, d_send, d_recv,
     fx_send, fx_recv, fd_send, fd_recv, give_send, give_recv, pair_send, pair_recv,
     act_send, act_recv, term_send, term_recv, dx_send, dx_recv, back_send, back_recv,
 ):
@@ -208,10 +208,14 @@
         return copy
 
     small = [local(ids, named, in_sem.at[2]), local(route, paid, in_sem.at[3])]
-    weights = (wg, wu, wd)
-    own_w = [local(w, w_all.at[i, 0], w_local.at[i]) for i, w in enumerate(weights)]
-    tok_copy = local(tokens, tok, in_sem.at[0])
-    ogr_copy = local(out_grad, ogr, in_sem.at[1])
+    order = (5, 6, 3, 4)
+    columns = [
+        pl.ds(pl.multiple_of(lax.rem(others[n], GROUP) * quarter, 128), quarter) for n in order
+    ]
+    tok_copies = [
+        local(tokens.at[:, at], tok.at[:, at], tok_sem.at[n]) for n, at in enumerate(columns)
+    ]
+    own_w = [local(wg, w_all.at[0, 0], w_local.at[0])]
 
     barrier = pltpu.get_barrier_semaphore()
     peers = [row_mate, weight_mate] + [(r, other) for other in others]
@@ -239,7 +243,26 @@
     scale[...] = jnp.sum(match * paid[...], axis=1, keepdims=True)
     pick_t[...] = match.T.astype(short)
 
-    pl.semaphore_wait(barrier, len(peers))
+    def by_quarters(fn):
+        def one(n, carry):
+            fn(pl.ds(pl.multiple_of(n * quarter, quarter), quarter))
+            return carry
+
+        lax.fori_loop(0, GROUP, one, 0)
+
+    def fill_x(at):
+        xs[:, at] = jnp.dot(
+            pick[...], tok[:, at], preferred_element_type=jnp.float32
+        ).astype(short)
+
+    def fill_d(at):
+        ds[:, at] = (
+            jnp.dot(pick[...], ogr[:, at], preferred_element_type=jnp.float32) * scale[...]
+        ).astype(short)
+
+    tok_copies[0].wait()
+    ogr_copy = local(out_grad, ogr, in_sem.at[1])
+    own_w += [local(w, w_all.at[i, 0], w_local.at[i]) for i, w in ((1, wu), (2, wd))]
 
     def remote(source, target, send, recv, peer, start=True):
         copy = pltpu.make_async_remote_copy(
@@ -250,60 +273,64 @@
             copy.start()
         return copy
 
-    def owned(ref, device):
-        row = pl.multiple_of(lax.div(device, GROUP) * capacity, capacity)
+    def owned(ref, device, part=slice(None)):
+        first, size = (0, capacity) if part == slice(None) else part
+        row = pl.multiple_of(lax.div(device, GROUP) * capacity, 16) + first
         column = pl.multiple_of(lax.rem(device, GROUP) * quarter, 128)
-        return ref.at[pl.ds(row, capacity), pl.ds(column, quarter)]
+        return ref.at[pl.ds(pl.multiple_of(row, 16), size), pl.ds(column, quarter)]
 
     w_copies = []
-    for i in range(3):
-        own_w[i].wait()
+
+    def send_weight(i):
+        if i:
+            own_w[i].wait()
         w_copies.append(
-            remote(w_all.at[i, 0], w_all.at[i, 1], w_send.at[i], w_recv.at[i], weight_mate)
-        )
-
-    def by_quarters(fn):
-        def one(n, carry):
-            fn(pl.ds(pl.multiple_of(n * quarter, quarter), quarter))
-            return carry
-
-        lax.fori_loop(0, GROUP, one, 0)
-
-    def fill_x(at):
-        xs[:, at] = jnp.dot(
-            pick[...], tok[:, at], preferred_element_type=jnp.float32
-        ).astype(short)
-
-    def fill_d(at):
-        ds[:, at] = (
-            jnp.dot(pick[...], ogr[:, at], preferred_element_type=jnp.float32) * scale[...]
-        ).astype(short)
-
+            remote(w_all.at[i, 0], w_all.at[i, 1], w_send.at[0], w_recv.at[i], weight_mate)
+        )
+
+    LAST = 16
+    WHOLE = ((0, capacity),)
+    SPLIT = ((0, capacity - LAST), (capacity - LAST, LAST))
     kinds = ((xs, x_all, x_send, x_recv), (ds, d_all, d_send, d_recv))
 
-    def flow(kind, n):
+    def parts_of(kind, n):
+        return SPLIT if kind and n is not None and n in FAR else WHOLE
+
+    def flow(kind, n, piece):
         source, target, send, recv = kinds[kind]
         peer = others[n]
+        part = parts_of(kind, n)[piece]
         return remote(
-            owned(source, peer), target.at[0, s], send.at[n], recv.at[s], (r, peer), start=False
+            owned(source, peer, part), target.at[0, s, pl.ds(*part)], send.at[0],
+            recv.at[piece, s], (r, peer), start=False,
         )
 
     def send(kind, which):
         for n in which:
-            flow(kind, n).start()
+            for piece in range(len(parts_of(kind, n))):
+                flow(kind, n, piece).start()
 
     self_copies = []
-    tok_copy.wait()
-    by_quarters(fill_x)
+
+    fill_x(columns[0])
+    own_w[0].wait()
+    pl.semaphore_wait(barrier, len(peers))
+    send_weight(0)
+    for n, peer in enumerate(order):
+        if n:
+            tok_copies[n].wait()
+            fill_x(columns[n])
+
+        @pl.when(jnp.logical_not(at_end))
+        def _(peer=peer):
+            send(0, (peer,))
+
     send(0, CORE + NEAR)
     self_copies.append(local(owned(xs, s), x_all.at[0, s], self_sem.at[0]))
-
-    @pl.when(jnp.logical_not(at_end))
-    def _():
-        send(0, FAR)
-
     ogr_copy.wait()
     by_quarters(fill_d)
+    send_weight(1)
+    send_weight(2)
     send(1, CORE + NEAR)
     self_copies.append(local(owned(ds, s), d_all.at[0, s], self_sem.at[1]))
 
@@ -311,26 +338,27 @@
     def _():
         send(0, FAR)
 
-    passed = ([], [])
-
-    def pass_on(kind, n):
+    def landed(ref, sem):
+        pltpu.make_async_copy(ref, ref, sem.at[0]).wait()
+
+
+    def pass_on(kind, n, at_middle=None):
         _, target, _, recv = kinds[kind]
+        origin = s if n is None else others[n]
+        if at_middle is not None:
+            origin = end * origin + (1 - end) * others[at_middle]
+        to_send, to_recv = ((fx_send, fx_recv), (fd_send, fd_recv))[kind]
         if n is None:
-            origin = s
             self_copies[kind].wait()
-        else:
-            origin = others[n]
+        for piece, part in enumerate(parts_of(kind, n)):
+            here = target.at[0, origin, pl.ds(*part)]
+            if n is not None:
+                remote(
+                    here, here, x_send.at[0], recv.at[piece, origin], (r, origin), start=False
+                ).wait_recv()
             remote(
-                target.at[0, origin], target.at[0, origin], x_send.at[0], recv.at[origin],
-                (r, origin), start=False,
-            ).wait_recv()
-        to_send, to_recv = ((fx_send, fx_recv), (fd_send, fd_recv))[kind]
-        passed[kind].append(
-            remote(
-                target.at[0, origin], target.at[1, origin], to_send.at[origin],
-                to_recv.at[origin], row_mate,
+                here, target.at[1, origin, pl.ds(*part)], to_send.at[0], to_recv.at[0], row_mate
             )
-        )
 
     def project(k, i):
         block = (x_all if i < 2 else d_all)[k].reshape(rows, quarter)
@@ -352,7 +380,7 @@
     def hand_over(k, i):
         give_copies[k, i] = remote(
             part.at[k, 1 - core, i], got.at[k, i],
-            give_send.at[3 * k + i], give_recv.at[3 * k + i], core_mate,
+            give_send.at[0], give_recv.at[3 * k + i], core_mate,
         )
 
     def send_pair(k, i):
@@ -366,7 +394,7 @@
         by_rows(add_pair)
         pair_copies[k, i] = remote(
             pair.at[k, i], across.at[k, i],
-            pair_send.at[3 * k + i], pair_recv.at[3 * k + i], chip_mate,
+            pair_send.at[0], pair_recv.at[3 * k + i], chip_mate,
         )
 
     def total(k, i, at):
@@ -383,7 +411,7 @@
         by_rows(one)
         act_copies[k, 0] = remote(
             act.at[k, core, 0], act.at[k, core, 0],
-            act_send.at[2 * k], act_recv.at[2 * k], core_mate,
+            act_send.at[0], act_recv.at[2 * k], core_mate,
         )
 
     def make_slopes(k):
@@ -397,7 +425,7 @@
         by_rows(one)
         act_copies[k, 1] = remote(
             act.at[k, core, pl.ds(1, 2)], act.at[k, core, pl.ds(1, 2)],
-            act_send.at[2 * k + 1], act_recv.at[2 * k + 1], core_mate,
+            act_send.at[0], act_recv.at[2 * k + 1], core_mate,
         )
 
     def transpose(which, piece):
@@ -420,7 +448,8 @@
         )
 
     CUTS = 2
-    cuts = [pl.ds(n * (hidden // CUTS), hidden // CUTS) for n in range(CUTS)]
+    FIRST = hidden // 4
+    cuts = [pl.ds(0, FIRST), pl.ds(FIRST, hidden - FIRST)]
     term_copies = {}
 
     def send_term(i):
@@ -432,7 +461,7 @@
             by_columns(make)
             term_copies[i, n] = remote(
                 term_out.at[i, cut], term_in.at[i, cut],
-                term_send.at[CUTS * i + n], term_recv.at[CUTS * i + n], weight_mate,
+                term_send.at[0], term_recv.at[CUTS * i + n], weight_mate,
             )
 
     def own_term(i):
@@ -472,7 +501,7 @@
             block = dx_blocks[n]
             dx_copies.append(
                 remote(
-                    dx_out.at[block], dx_in.at[block], dx_send.at[n], dx_recv.at[n], row_mate
+                    dx_out.at[block], dx_in.at[block], dx_send.at[0], dx_recv.at[n], row_mate
                 )
             )
 
@@ -493,7 +522,7 @@
         if n < devices_ep - 1:
             backs.append(
                 remote(
-                    dx_sum.at[block], owned(slot_rows, s), back_send.at[n], back_recv.at[s],
+                    dx_sum.at[block], owned(slot_rows, s), back_send.at[0], back_recv.at[0],
                     (r, block),
                 )
             )
@@ -504,8 +533,12 @@
         pass_on(kind, None)
         for n in CORE:
             pass_on(kind, n)
-    for n in (1, 2, 5, 6, 3, 4):
-        pass_on(0, n)
+    pass_on(0, 1)
+    pass_on(0, 2)
+    pass_on(0, 5)
+    pass_on(0, 6)
+    pass_on(0, 3)
+    pass_on(0, 4)
 
     @pl.when(jnp.logical_not(at_end))
     def _():
@@ -513,7 +546,7 @@
 
     @pl.when(at_end)
     def _():
-        send(1, (3, 4))
+        send(1, (3, 5))
 
     for n in NEAR:
         pass_on(1, n)
@@ -524,10 +557,9 @@
 
     @pl.when(at_end)
     def _():
-        send(1, (5,))
-
-    for copy in passed[0]:
-        copy.wait_recv()
+        send(1, (6,))
+
+    landed(x_all.at[1], fx_recv)
     project(1, 0)
     hand_over(1, 0)
     w_copies[1].wait_recv()
@@ -540,22 +572,23 @@
 
     @pl.when(at_end)
     def _():
-        send(1, (6,))
+        send(1, (4,))
 
     send_pair(1, 1)
-    for n in (3, 5, 4, 6):
-        pass_on(1, n)
+    pass_on(1, 3)
+    pass_on(1, 5, 4)
+    pass_on(1, 6, 5)
+    pass_on(1, 4, 6)
+    make_hidden(0)
     w_copies[2].wait_recv()
     project(0, 2)
     hand_over(0, 2)
-    make_hidden(0)
     make_hidden(1)
     send_pair(0, 2)
     for k in range(2):
         act_copies[k, 0].wait_recv()
     transpose(1, 0)
-    for copy in passed[1]:
-        copy.wait_recv()
+    landed(d_all.at[1], fd_recv)
     send_term(2)
     project(1, 2)
     hand_over(1, 2)
@@ -585,38 +618,41 @@
         give_back(n)
     finish(0)
     backs[-1].wait()
-    for origin in others:
-        remote(
-            dx_sum.at[0], owned(slot_rows, origin), back_send.at[0], back_recv.at[origin],
-            (r, origin), start=False,
-        ).wait_recv()
-
-    def fill_in(at):
-        in_grad[:, at] = jnp.dot(
-            pick_t[...], slot_rows[:, at], preferred_element_type=jnp.float32
+    landed(dx_sum.at[pl.ds(0, devices_ep - 1)], back_recv)
+
+    for n, out in enumerate((in_0, in_1, in_2, in_3)):
+        out[...] = jnp.dot(
+            pick_t[...], slot_rows[:, n * quarter : (n + 1) * quarter],
+            preferred_element_type=jnp.float32,
         ).astype(short)
-
-    by_quarters(fill_in)
     finish(1)
-    for kind in range(2):
-        for n in range(devices_ep - 1):
-            flow(kind, n).wait_send()
-    sent = w_copies + passed[0] + passed[1] + list(give_copies.values())
-    sent += list(pair_copies.values()) + list(act_copies.values())
-    sent += list(term_copies.values()) + dx_copies + backs[:-1]
-    for copy in sent:
-        copy.wait_send()
+    most = pl.ds(0, devices_ep - 1)
+    for sem in (x_send, d_send, back_send):
+        landed(dx_sum.at[most], sem)
+    for sem in (fx_send, fd_send, dx_send):
+        landed(dx_sum, sem)
+    for sem in (give_send, pair_send, act_send):
+        landed(got, sem)
+    for sem in (w_send, term_send):
+        landed(term_in, sem)
 
 
 def store_kernel(*refs):
-    count = len(refs) // 2
-    copies = [
-        pltpu.make_async_copy(refs[i], refs[count + i], refs[-1].at[i]) for i in range(count)
+    grads = refs[GROUP : GROUP + 3]
+    whole, outs, sem = refs[GROUP + 3], refs[GROUP + 4 : GROUP + 7], refs[-1]
+    quarter = whole.shape[1] // GROUP
+    stores = [
+        pltpu.make_async_copy(part, whole.at[:, pl.ds(n * quarter, quarter)], sem.at[n])
+        for n, part in enumerate(refs[:GROUP])
     ]
-    for copy in copies:
-        copy.start()
-    for copy in copies:
-        copy.wait()
+    stores += [
+        pltpu.make_async_copy(grad, out, sem.at[GROUP + n])
+        for n, (grad, out) in enumerate(zip(grads, outs))
+    ]
+    for store in stores:
+        store.start()
+    for store in stores:
+        store.wait()
 
 
 def fast_body(tokens, out_grad, route_weight, expert_ids, w_gate, w_up, w_down):
@@ -635,9 +671,9 @@
     dma = pltpu.SemaphoreType.DMA
     results = pl.pallas_call(
         expert_kernel,
-        out_shape=(jax.ShapeDtypeStruct(tokens.shape, short), grad, grad, grad),
+        out_shape=(jax.ShapeDtypeStruct((token_count, quarter), short),) * GROUP + (grad,) * 3,
         in_specs=[far] * 7,
-        out_specs=(vmem, vmem, vmem, vmem),
+        out_specs=(vmem,) * (GROUP + 3),
         scratch_shapes=[
             pltpu.VMEM((1, token_count), jnp.int32),
             pltpu.VMEM((1, token_count), jnp.float32),
@@ -666,15 +702,14 @@
             pltpu.VMEM((devices_ep, capacity, quarter), jnp.float32),
             pltpu.VMEM((devices_ep, capacity, quarter), short),
         ]
-        + [dma((4,))]
-        + [dma((3,))] * 4
-        + [dma((devices_ep,))] * 8
-        + [dma((6,))] * 4
-        + [dma((4,))] * 2
-        + [dma((6,))] * 2
-        + [dma((devices_ep,))] * 4,
+        + [dma((4,)), dma((GROUP,)), dma((3,)), dma((1,)), dma((3,)), dma((3,))]
+        + [dma((1,)), dma((1, devices_ep)), dma((1,)), dma((2, devices_ep))]
+        + [dma((1,))] * 4
+        + [dma((1,)), dma((6,))] * 2
+        + [dma((1,)), dma((4,)), dma((1,)), dma((6,)), dma((1,)), dma((devices_ep,))]
+        + [dma((1,))] * 2,
         compiler_params=pltpu.CompilerParams(
-            collective_id=0, has_side_effects=True, vmem_limit_bytes=52 * 2**20
+            collective_id=0, has_side_effects=True, vmem_limit_bytes=51904512
         ),
     )(
         tokens, out_grad, route_weight.reshape(1, token_count),
@@ -683,11 +718,11 @@
     return tuple(
         pl.pallas_call(
             store_kernel,
-            out_shape=tuple(jax.ShapeDtypeStruct(v.shape, v.dtype) for v in results),
+            out_shape=(jax.ShapeDtypeStruct(tokens.shape, short), grad, grad, grad),
             in_specs=[vmem] * len(results),
-            out_specs=(far,) * len(results),
+            out_specs=(far,) * 4,
             scratch_shapes=[dma((len(results),))],
-            compiler_params=pltpu.CompilerParams(vmem_limit_bytes=8 * 2**20),
+            compiler_params=pltpu.CompilerParams(vmem_limit_bytes=40 * 2**20),
         )(*results)
     )
 

time: 145 us -> 139 us (0.959)
  local copies, waits for them, and re-layouts: 3.97 us -> 1.3 us
  Pallas kernels: 139 us -> 137 us
    unnamed x8 -> x4, local copies, waits for them, and re-layouts: 3.97 us -> 1.3 us
    pallas_call x2, Pallas kernels: 139 us -> 137 us  [the longest x1 135 us: fast_body(): pl.pallas_call(expert_kernel, out_shape=(jax.ShapeDtypeStruct((token_coun...]
where the time goes in v3:
time: 139 us
  Pallas kernels  137 us (99%)
    pallas_call x1, Pallas kernels, fast_body(): pl.pallas_call(expert_kernel, out_shape=(jax.ShapeDtypeStruct((token_coun...  135 us

profile of v3, /device:TPU:0, one launch (start us, length us, event | category | flops | bytes accessed | tf_op | source)
XLA Modules:
  0.0 139.1 jit_solution(17171794951162615684)
XLA Ops:
  0.6 0.0 copy-start
  0.6 0.6 copy-done
  1.3 0.0 copy-start.1
  1.3 0.7 copy-done.1
  1.9 135.0 %shard_map.102 = (bf16[128,1792]{1,0:T(8,128)(2,1)S(1)}, bf16[128,1792]{1,0:T(8,128)(2,1)S(1)}, bf16[128,1792]{1,0:T(8,128)(2,1)S(1)}, bf16[128,1792]{1,0:T(8,12...) custom-call(bf16[128,7168]{1,0:T(8,128)(2,1)} %tokens.1, ...), custom_call_target="tpu_custom_call" | custom-call | tf_op jit(solution)/shard_map/pallas_call | solution.py:672
  136.9 2.2 %shard_map.103 = (bf16[128,7168]{1,0:T(8,128)(2,1)}, bf16[256,1792]{1,0:T(8,128)(2,1)}, bf16[256,1792]{1,0:T(8,128)(2,1)}, bf16[256,1792]{1,0:T(8,128)(2,1)}) custom-call(bf16[128,1792]{1,0:T(8,128)(2,1)S(1)} %get-tuple-element.11.refs_0_, bf16[128,1792]{1,0:T(8,128)(2,1)S(1)} %get-tuple-element.12.refs_1_, bf16[128,1792]{1,0:T(8,128)(2,1)S(1)} %get-tuple-element.13.refs_2_, ...), custom_call_target="tpu_custom_call" | custom-call | tf_op jit(solution)/shard_map/pallas_call | solution.py:719
Async XLA Ops:
  0.6 0.7 copy-start
  1.3 0.7 copy-start.1

commit v4 on v3

--- a/solution.py
+++ b/solution.py
@@ -288,9 +288,9 @@
             remote(w_all.at[i, 0], w_all.at[i, 1], w_send.at[0], w_recv.at[i], weight_mate)
         )
 
-    LAST = 16
+    SLICE = 16
     WHOLE = ((0, capacity),)
-    SPLIT = ((0, capacity - LAST), (capacity - LAST, LAST))
+    SPLIT = tuple((first, SLICE) for first in range(0, capacity, SLICE))
     kinds = ((xs, x_all, x_send, x_recv), (ds, d_all, d_send, d_recv))
 
     def parts_of(kind, n):
@@ -529,11 +529,10 @@
         else:
             backs.append(local(dx_sum.at[block], owned(slot_rows, s), self_sem.at[2]))
 
-    for kind in range(2):
-        pass_on(kind, None)
-        for n in CORE:
-            pass_on(kind, n)
+    pass_on(0, None)
+    pass_on(0, 0)
     pass_on(0, 1)
+    pass_on(1, None)
     pass_on(0, 2)
     pass_on(0, 5)
     pass_on(0, 6)
@@ -548,7 +547,7 @@
     def _():
         send(1, (3, 5))
 
-    for n in NEAR:
+    for n in CORE + NEAR:
         pass_on(1, n)
     w_copies[0].wait_recv()
     project(0, 0)
@@ -562,10 +561,10 @@
     landed(x_all.at[1], fx_recv)
     project(1, 0)
     hand_over(1, 0)
+    send_pair(1, 0)
     w_copies[1].wait_recv()
     project(0, 1)
     hand_over(0, 1)
-    send_pair(1, 0)
     project(1, 1)
     hand_over(1, 1)
     send_pair(0, 1)
@@ -703,17 +702,22 @@
             pltpu.VMEM((devices_ep, capacity, quarter), short),
         ]
         + [dma((4,)), dma((GROUP,)), dma((3,)), dma((1,)), dma((3,)), dma((3,))]
-        + [dma((1,)), dma((1, devices_ep)), dma((1,)), dma((2, devices_ep))]
+        + [dma((1,)), dma((1, devices_ep)), dma((1,)), dma((capacity // 16, devices_ep))]
         + [dma((1,))] * 4
         + [dma((1,)), dma((6,))] * 2
         + [dma((1,)), dma((4,)), dma((1,)), dma((6,)), dma((1,)), dma((devices_ep,))]
         + [dma((1,))] * 2,
         compiler_params=pltpu.CompilerParams(
-            collective_id=0, has_side_effects=True, vmem_limit_bytes=51904512
+            collective_id=0, has_side_effects=True, vmem_limit_bytes=48 * 2**20
         ),
     )(
-        tokens, out_grad, route_weight.reshape(1, token_count),
-        expert_ids.reshape(1, token_count), w_gate, w_up, w_down,
+        *(
+            pltpu.with_memory_space_constraint(value, pltpu.HBM)
+            for value in (
+                tokens, out_grad, route_weight.reshape(1, token_count),
+                expert_ids.reshape(1, token_count), w_gate, w_up, w_down,
+            )
+        )
     )
     return tuple(
         pl.pallas_call(

time: 139 us -> 137 us (0.986)
  no operation moved by 1% of the time
where the time goes in v4:
time: 137 us
  Pallas kernels  136 us (99%)
    pallas_call x1, Pallas kernels, fast_body(): pl.pallas_call(expert_kernel, out_shape=(jax.ShapeDtypeStruct((token_coun...  134 us

profile of v4, /device:TPU:0, one launch (start us, length us, event | category | flops | bytes accessed | tf_op | source)
XLA Modules:
  0.0 136.7 jit_solution(10566781417249493116)
XLA Ops:
  0.6 133.8 %shard_map.102 = (bf16[128,1792]{1,0:T(8,128)(2,1)S(1)}, bf16[128,1792]{1,0:T(8,128)(2,1)S(1)}, bf16[128,1792]{1,0:T(8,128)(2,1)S(1)}, bf16[128,1792]{1,0:T(8,12...) custom-call(bf16[128,7168]{1,0:T(8,128)(2,1)} %tokens.1, ...), custom_call_target="tpu_custom_call" | custom-call | tf_op jit(solution)/shard_map/pallas_call | solution.py:671
  134.5 2.2 %shard_map.103 = (bf16[128,7168]{1,0:T(8,128)(2,1)}, bf16[256,1792]{1,0:T(8,128)(2,1)}, bf16[256,1792]{1,0:T(8,128)(2,1)}, bf16[256,1792]{1,0:T(8,128)(2,1)}) custom-call(bf16[128,1792]{1,0:T(8,128)(2,1)S(1)} %get-tuple-element.11.refs_0_, bf16[128,1792]{1,0:T(8,128)(2,1)S(1)} %get-tuple-element.12.refs_1_, bf16[128,1792]{1,0:T(8,128)(2,1)S(1)} %get-tuple-element.13.refs_2_, ...), custom_call_target="tpu_custom_call" | custom-call | tf_op jit(solution)/shard_map/pallas_call | solution.py:723

commit v5 on v4

--- a/solution.py
+++ b/solution.py
@@ -215,7 +215,15 @@
     tok_copies = [
         local(tokens.at[:, at], tok.at[:, at], tok_sem.at[n]) for n, at in enumerate(columns)
     ]
-    own_w = [local(wg, w_all.at[0, 0], w_local.at[0])]
+    small_half = hidden // 2
+
+    def load_weight(i, w):
+        for half in range(2):
+            local(
+                w.at[pl.ds(half * small_half, small_half)], w_all.at[i, half, 0], w_local.at[i]
+            )
+
+    load_weight(0, wg)
 
     barrier = pltpu.get_barrier_semaphore()
     peers = [row_mate, weight_mate] + [(r, other) for other in others]
@@ -262,7 +270,8 @@
 
     tok_copies[0].wait()
     ogr_copy = local(out_grad, ogr, in_sem.at[1])
-    own_w += [local(w, w_all.at[i, 0], w_local.at[i]) for i, w in ((1, wu), (2, wd))]
+    load_weight(1, wu)
+    load_weight(2, wd)
 
     def remote(source, target, send, recv, peer, start=True):
         copy = pltpu.make_async_remote_copy(
@@ -279,13 +288,16 @@
         column = pl.multiple_of(lax.rem(device, GROUP) * quarter, 128)
         return ref.at[pl.ds(pl.multiple_of(row, 16), size), pl.ds(column, quarter)]
 
+    def landed(ref, sem):
+        pltpu.make_async_copy(ref, ref, sem.at[0]).wait()
+
     w_copies = []
 
     def send_weight(i):
         if i:
-            own_w[i].wait()
+            landed(w_all.at[i, :, 0], w_local.at[pl.ds(i, 1)])
         w_copies.append(
-            remote(w_all.at[i, 0], w_all.at[i, 1], w_send.at[0], w_recv.at[i], weight_mate)
+            remote(w_all.at[i, :, 0], w_all.at[i, :, 1], w_send.at[0], w_recv.at[i], weight_mate)
         )
 
     SLICE = 16
@@ -313,7 +325,7 @@
     self_copies = []
 
     fill_x(columns[0])
-    own_w[0].wait()
+    landed(w_all.at[0, :, 0], w_local)
     pl.semaphore_wait(barrier, len(peers))
     send_weight(0)
     for n, peer in enumerate(order):
@@ -337,9 +349,6 @@
     @pl.when(at_end)
     def _():
         send(0, FAR)
-
-    def landed(ref, sem):
-        pltpu.make_async_copy(ref, ref, sem.at[0]).wait()
 
 
     def pass_on(kind, n, at_middle=None):
@@ -363,8 +372,8 @@
     def project(k, i):
         block = (x_all if i < 2 else d_all)[k].reshape(rows, quarter)
         both = dot_last(block, w_all[i].reshape(2 * hidden, quarter)).astype(short)
-        for which in range(2):
-            part[k, which, i] = both[:, which * hidden : (which + 1) * hidden]
+        for half in range(2):
+            part[k, half, i] = both[:, half * hidden : (half + 1) * hidden]
 
     STEP = 48
 
@@ -414,6 +423,10 @@
             act_send.at[0], act_recv.at[2 * k], core_mate,
         )
 
+    def take_hidden():
+        for k in range(2):
+            act_copies[k, 0].wait_recv()
+
     def make_slopes(k):
         pair_copies[k, 2].wait_recv()
 
@@ -428,9 +441,9 @@
             act_send.at[0], act_recv.at[2 * k + 1], core_mate,
         )
 
-    def transpose(which, piece):
+    def transpose(half, piece):
         for k in range(2):
-            act_t[which, piece, :, k * rows : (k + 1) * rows] = act[k, which, piece].T
+            act_t[half, piece, :, k * rows : (k + 1) * rows] = act[k, half, piece].T
 
     LANES = 896
 
@@ -441,32 +454,39 @@
 
         lax.fori_loop(0, quarter // LANES, one, 0)
 
-    def term(which, i, cut, at):
+    def term(which, i, half, at, first=0, size=small_half):
         block = (x_all if i < 2 else d_all)[:, :, :, at].reshape(2 * rows, LANES)
+        units = pl.ds(which * small_half + first, size)
         return jnp.dot(
-            act_t[which, (i + 1) % 3, cut, :], block, preferred_element_type=jnp.float32
-        )
-
-    CUTS = 2
-    FIRST = hidden // 4
-    cuts = [pl.ds(0, FIRST), pl.ds(FIRST, hidden - FIRST)]
+            act_t[half, (i + 1) % 3, units, :], block, preferred_element_type=jnp.float32
+        )
+
+    FIRST = small_half // 2
+    spans = [(core, 0, FIRST), (core, FIRST, small_half - FIRST), (1 - core, 0, small_half)]
+    cuts = [
+        pl.ds(pl.multiple_of(half * small_half, small_half) + first, size)
+        for half, first, size in spans
+    ]
     term_copies = {}
 
-    def send_term(i):
-        for n, cut in enumerate(cuts):
-
-            def make(at, cut=cut):
-                term_out[i, cut, at] = term(1, i, cut, at).astype(short)
-
-            by_columns(make)
-            term_copies[i, n] = remote(
-                term_out.at[i, cut], term_in.at[i, cut],
-                term_send.at[0], term_recv.at[CUTS * i + n], weight_mate,
-            )
+    def send_term(i, n):
+        (half, first, size), cut = spans[n], cuts[n]
+
+        def make(at):
+            term_out[i, cut, at] = term(1, i, half, at, first, size).astype(short)
+
+        by_columns(make)
+        term_copies[i, n] = remote(
+            term_out.at[i, cut], term_in.at[i, cut],
+            term_send.at[0], term_recv.at[len(cuts) * i + n], weight_mate,
+        )
 
     def own_term(i):
         def make(at):
-            term_own[i, :, at] = term(0, i, slice(None), at)
+            for half in range(2):
+                term_own[i, half * small_half : (half + 1) * small_half, at] = term(
+                    0, i, half, at
+                )
 
         by_columns(make)
 
@@ -480,10 +500,10 @@
         here = pl.ds(pl.multiple_of(part_of * half_rows, half_rows), half_rows)
         return sum(
             jnp.dot(
-                act[k, which, i + 1, here, :], w_all[i, which, :, at],
+                act[k, half, i + 1, here, :], w_all[i, half, :, :, at].reshape(hidden, LANES),
                 preferred_element_type=jnp.float32,
             )
-            for which in range(2)
+            for half in range(2)
             for i in range(2)
         ).reshape(devices_ep // 2, capacity, LANES)
 
@@ -583,15 +603,16 @@
     project(0, 2)
     hand_over(0, 2)
     make_hidden(1)
+    transpose(core, 0)
+    landed(d_all.at[1], fd_recv)
+    send_term(2, 0)
+    send_term(2, 1)
     send_pair(0, 2)
-    for k in range(2):
-        act_copies[k, 0].wait_recv()
-    transpose(1, 0)
-    landed(d_all.at[1], fd_recv)
-    send_term(2)
+    take_hidden()
+    transpose(1 - core, 0)
+    send_term(2, 2)
     project(1, 2)
     hand_over(1, 2)
-    transpose(0, 0)
     send_pair(1, 2)
     own_term(2)
     make_slopes(0)
@@ -600,18 +621,17 @@
     act_copies[1, 1].wait_recv()
     send_dx(1 - side, range(0, 4))
     send_dx(side, range(4, 8))
-    transpose(1, 1)
-    send_term(0)
-    transpose(1, 2)
-    send_term(1)
+    for i in range(2):
+        for half in range(2):
+            transpose(half, i + 1)
+        for n in range(len(cuts)):
+            send_term(i, n)
     own_dx(1 - side)
     for n in range(4):
         give_back(n)
     own_dx(side)
     finish(2)
-    transpose(0, 1)
     own_term(0)
-    transpose(0, 2)
     own_term(1)
     for n in range(4, 8):
         give_back(n)
@@ -686,7 +706,7 @@
             pltpu.VMEM((slots, D), short),
             pltpu.VMEM((2, devices_ep, capacity, quarter), short),
             pltpu.VMEM((2, devices_ep, capacity, quarter), short),
-            pltpu.VMEM((3, 2, hidden, quarter), short),
+            pltpu.VMEM((3, 2, 2, hidden // 2, quarter), short),
             pltpu.VMEM((2, 2, 3, rows, hidden), short),
             pltpu.VMEM((2, 3, rows, hidden), short),
             pltpu.VMEM((2, 3, rows, hidden), short),
@@ -705,7 +725,7 @@
         + [dma((1,)), dma((1, devices_ep)), dma((1,)), dma((capacity // 16, devices_ep))]
         + [dma((1,))] * 4
         + [dma((1,)), dma((6,))] * 2
-        + [dma((1,)), dma((4,)), dma((1,)), dma((6,)), dma((1,)), dma((devices_ep,))]
+        + [dma((1,)), dma((4,)), dma((1,)), dma((9,)), dma((1,)), dma((devices_ep,))]
         + [dma((1,))] * 2,
         compiler_params=pltpu.CompilerParams(
             collective_id=0, has_side_effects=True, vmem_limit_bytes=48 * 2**20
@@ -738,7 +758,7 @@
         token_count = arrays[0].shape[0]
         capacity = 6 * GROUP * token_count * TOP // (8 * devices_ep)
         hidden = arrays[4].shape[0]
-        fits = capacity % 48 == 0 and hidden % 128 == 0 and token_count % 128 == 0
+        fits = capacity % 48 == 0 and hidden % 256 == 0 and token_count % 128 == 0
         fits = fits and mesh.shape["dp"] == 4 and devices_ep == 2 * GROUP
         return (fast_body if fits else body)(*arrays)
 

time: 137 us -> 136 us (level)
  no operation moved by 1% of the time
where the time goes in v5:
time: 136 us; the launch traced here: 135 us
  Pallas kernels  135 us (99%)
    pallas_call x1, Pallas kernels, fast_body(): pl.pallas_call(expert_kernel, out_shape=(jax.ShapeDtypeStruct((token_coun...  133 us

profile of v5, /device:TPU:0, one launch (start us, length us, event | category | flops | bytes accessed | tf_op | source)
XLA Modules:
  0.0 135.4 jit_solution(14084216117611731073)
XLA Ops:
  0.6 132.6 %shard_map.102 = (bf16[128,1792]{1,0:T(8,128)(2,1)S(1)}, bf16[128,1792]{1,0:T(8,128)(2,1)S(1)}, bf16[128,1792]{1,0:T(8,128)(2,1)S(1)}, bf16[128,1792]{1,0:T(8,12...) custom-call(bf16[128,7168]{1,0:T(8,128)(2,1)} %tokens.1, ...), custom_call_target="tpu_custom_call" | custom-call | tf_op jit(solution)/shard_map/pallas_call | solution.py:691
  133.2 2.2 %shard_map.103 = (bf16[128,7168]{1,0:T(8,128)(2,1)}, bf16[256,1792]{1,0:T(8,128)(2,1)}, bf16[256,1792]{1,0:T(8,128)(2,1)}, bf16[256,1792]{1,0:T(8,128)(2,1)}) custom-call(bf16[128,1792]{1,0:T(8,128)(2,1)S(1)} %get-tuple-element.11.refs_0_, bf16[128,1792]{1,0:T(8,128)(2,1)S(1)} %get-tuple-element.12.refs_1_, bf16[128,1792]{1,0:T(8,128)(2,1)S(1)} %get-tuple-element.13.refs_2_, ...), custom_call_target="tpu_custom_call" | custom-call | tf_op jit(solution)/shard_map/pallas_call | solution.py:743

commit v6 on v5

--- a/solution.py
+++ b/solution.py
@@ -179,7 +179,7 @@
     act, act_t, term_out, term_in, term_own, dx_out, dx_in, dx_own, dx_sum,
     in_sem, tok_sem, w_local, w_send, w_recv, self_sem, x_send, x_recv, d_send, d_recv,
     fx_send, fx_recv, fd_send, fd_recv, give_send, give_recv, pair_send, pair_recv,
-    act_send, act_recv, term_send, term_recv, dx_send, dx_recv, back_send, back_recv,
+    side_send, side_recv, act_send, act_recv, term_send, term_recv, dx_send, dx_recv, back_send, back_recv,
 ):
     devices_ep, capacity, quarter = dx_sum.shape
     rows = devices_ep * capacity
@@ -384,7 +384,17 @@
 
         lax.fori_loop(0, rows // STEP, one, 0)
 
-    give_copies, pair_copies, act_copies = {}, {}, {}
+    def by_my_rows(fn):
+        def one(n, carry):
+            fn(pl.ds(pl.multiple_of(mine * half_rows + n * STEP, STEP), STEP))
+            return carry
+
+        lax.fori_loop(0, half_rows // STEP, one, 0)
+
+    mine = lax.rem(z, 2)
+    my_rows = pl.ds(pl.multiple_of(mine * half_rows, half_rows), half_rows)
+    their_rows = pl.ds(pl.multiple_of((1 - mine) * half_rows, half_rows), half_rows)
+    give_copies, pair_copies, act_copies, side_copies = {}, {}, {}, {}
 
     def hand_over(k, i):
         give_copies[k, i] = remote(
@@ -402,12 +412,28 @@
 
         by_rows(add_pair)
         pair_copies[k, i] = remote(
-            pair.at[k, i], across.at[k, i],
+            pair.at[k, i, their_rows], across.at[k, i, their_rows],
             pair_send.at[0], pair_recv.at[3 * k + i], chip_mate,
         )
 
     def total(k, i, at):
         return wide(pair[k, i, at, :]) + wide(across[k, i, at, :])
+
+    def share(k, stage, pieces):
+        here = act.at[k, core, pieces, my_rows]
+        side_copies[k, stage] = remote(
+            here, here, side_send.at[0], side_recv.at[3 * k + stage], chip_mate
+        )
+        act_copies[k, stage, 0] = remote(
+            here, here, act_send.at[0], act_recv.at[6 * k + 2 * stage], core_mate
+        )
+
+    def take_side(k, stage, pieces):
+        side_copies[k, stage].wait_recv()
+        here = act.at[k, core, pieces, their_rows]
+        act_copies[k, stage, 1] = remote(
+            here, here, act_send.at[0], act_recv.at[6 * k + 2 * stage + 1], core_mate
+        )
 
     def make_hidden(k):
         for i in range(2):
@@ -417,15 +443,13 @@
             gate, up = total(k, 0, at), total(k, 1, at)
             act[k, core, 0, at, :] = (gate * jax.nn.sigmoid(gate) * up).astype(short)
 
-        by_rows(one)
-        act_copies[k, 0] = remote(
-            act.at[k, core, 0], act.at[k, core, 0],
-            act_send.at[0], act_recv.at[2 * k], core_mate,
-        )
-
-    def take_hidden():
+        by_my_rows(one)
+        share(k, 0, pl.ds(0, 1))
+
+    def take(stage):
         for k in range(2):
-            act_copies[k, 0].wait_recv()
+            for n in range(2):
+                act_copies[k, stage, n].wait_recv()
 
     def make_slopes(k):
         pair_copies[k, 2].wait_recv()
@@ -435,11 +459,8 @@
             act[k, core, 1, at, :] = made[1]
             act[k, core, 2, at, :] = made[2]
 
-        by_rows(one)
-        act_copies[k, 1] = remote(
-            act.at[k, core, pl.ds(1, 2)], act.at[k, core, pl.ds(1, 2)],
-            act_send.at[0], act_recv.at[2 * k + 1], core_mate,
-        )
+        by_my_rows(one)
+        share(k, 1, pl.ds(1, 1))
 
     def transpose(half, piece):
         for k in range(2):
@@ -596,19 +617,31 @@
     send_pair(1, 1)
     pass_on(1, 3)
     pass_on(1, 5, 4)
-    pass_on(1, 6, 5)
-    pass_on(1, 4, 6)
+
+    @pl.when(at_end)
+    def _():
+        pass_on(1, 6, 5)
+        pass_on(1, 4, 6)
+
     make_hidden(0)
+    make_hidden(1)
+
+    @pl.when(jnp.logical_not(at_end))
+    def _():
+        pass_on(1, 6, 5)
+        pass_on(1, 4, 6)
+
     w_copies[2].wait_recv()
     project(0, 2)
     hand_over(0, 2)
-    make_hidden(1)
+    for k in range(2):
+        take_side(k, 0, pl.ds(0, 1))
     transpose(core, 0)
     landed(d_all.at[1], fd_recv)
     send_term(2, 0)
     send_term(2, 1)
     send_pair(0, 2)
-    take_hidden()
+    take(0)
     transpose(1 - core, 0)
     send_term(2, 2)
     project(1, 2)
@@ -617,15 +650,24 @@
     own_term(2)
     make_slopes(0)
     make_slopes(1)
-    act_copies[0, 1].wait_recv()
-    act_copies[1, 1].wait_recv()
+    for k in range(2):
+        share(k, 2, pl.ds(2, 1))
+    for k in range(2):
+        take_side(k, 1, pl.ds(1, 1))
+    take(1)
+    for half in range(2):
+        transpose(half, 1)
+    for n in range(len(cuts)):
+        send_term(0, n)
+    for k in range(2):
+        take_side(k, 2, pl.ds(2, 1))
+    take(2)
     send_dx(1 - side, range(0, 4))
     send_dx(side, range(4, 8))
-    for i in range(2):
-        for half in range(2):
-            transpose(half, i + 1)
-        for n in range(len(cuts)):
-            send_term(i, n)
+    for half in range(2):
+        transpose(half, 2)
+    for n in range(len(cuts)):
+        send_term(1, n)
     own_dx(1 - side)
     for n in range(4):
         give_back(n)
@@ -650,8 +692,10 @@
         landed(dx_sum.at[most], sem)
     for sem in (fx_send, fd_send, dx_send):
         landed(dx_sum, sem)
-    for sem in (give_send, pair_send, act_send):
+    for sem in (give_send, act_send):
         landed(got, sem)
+    for sem in (pair_send, side_send):
+        landed(got.at[0], sem)
     for sem in (w_send, term_send):
         landed(term_in, sem)
 
@@ -725,7 +769,7 @@
         + [dma((1,)), dma((1, devices_ep)), dma((1,)), dma((capacity // 16, devices_ep))]
         + [dma((1,))] * 4
         + [dma((1,)), dma((6,))] * 2
-        + [dma((1,)), dma((4,)), dma((1,)), dma((9,)), dma((1,)), dma((devices_ep,))]
+        + [dma((1,)), dma((6,)), dma((1,)), dma((12,)), dma((1,)), dma((9,)), dma((1,)), dma((devices_ep,))]
         + [dma((1,))] * 2,
         compiler_params=pltpu.CompilerParams(
             collective_id=0, has_side_effects=True, vmem_limit_bytes=48 * 2**20

time: 136 us -> 135 us (level)
  no operation moved by 1% of the time
where the time goes in v6:
time: 135 us
  Pallas kernels  134 us (99%)
    pallas_call x1, Pallas kernels, fast_body(): pl.pallas_call(expert_kernel, out_shape=(jax.ShapeDtypeStruct((token_coun...  132 us

profile of v6, /device:TPU:0, one launch (start us, length us, event | category | flops | bytes accessed | tf_op | source)
XLA Modules:
  0.0 134.6 jit_solution(8366021484452601244)
XLA Ops:
  0.6 131.6 %shard_map.102 = (bf16[128,1792]{1,0:T(8,128)(2,1)S(1)}, bf16[128,1792]{1,0:T(8,128)(2,1)S(1)}, bf16[128,1792]{1,0:T(8,128)(2,1)S(1)}, bf16[128,1792]{1,0:T(8,12...) custom-call(bf16[128,7168]{1,0:T(8,128)(2,1)} %tokens.1, ...), custom_call_target="tpu_custom_call" | custom-call | tf_op jit(solution)/shard_map/pallas_call | solution.py:735
  132.3 2.2 %shard_map.103 = (bf16[128,7168]{1,0:T(8,128)(2,1)}, bf16[256,1792]{1,0:T(8,128)(2,1)}, bf16[256,1792]{1,0:T(8,128)(2,1)}, bf16[256,1792]{1,0:T(8,128)(2,1)}) custom-call(bf16[128,1792]{1,0:T(8,128)(2,1)S(1)} %get-tuple-element.11.refs_0_, bf16[128,1792]{1,0:T(8,128)(2,1)S(1)} %get-tuple-element.12.refs_1_, bf16[128,1792]{1,0:T(8,128)(2,1)S(1)} %get-tuple-element.13.refs_2_, ...), custom_call_target="tpu_custom_call" | custom-call | tf_op jit(solution)/shard_map/pallas_call | solution.py:787

commit v7 on v6

--- a/solution.py
+++ b/solution.py
@@ -475,30 +475,33 @@
 
         lax.fori_loop(0, quarter // LANES, one, 0)
 
-    def term(which, i, half, at, first=0, size=small_half):
+    def term(which, i, half, at):
         block = (x_all if i < 2 else d_all)[:, :, :, at].reshape(2 * rows, LANES)
-        units = pl.ds(which * small_half + first, size)
+        units = pl.ds(which * small_half, small_half)
         return jnp.dot(
             act_t[half, (i + 1) % 3, units, :], block, preferred_element_type=jnp.float32
         )
 
-    FIRST = small_half // 2
-    spans = [(core, 0, FIRST), (core, FIRST, small_half - FIRST), (1 - core, 0, small_half)]
+    left, right = pl.ds(0, LANES), pl.ds(LANES, quarter - LANES)
+    spans = [(core, left), (core, right), (1 - core, pl.ds(0, quarter))]
     cuts = [
-        pl.ds(pl.multiple_of(half * small_half, small_half) + first, size)
-        for half, first, size in spans
+        (pl.ds(pl.multiple_of(half * small_half, small_half), small_half), columns_of)
+        for half, columns_of in spans
     ]
     term_copies = {}
 
     def send_term(i, n):
-        (half, first, size), cut = spans[n], cuts[n]
+        half, (rows_of, columns_of) = spans[n][0], cuts[n]
 
         def make(at):
-            term_out[i, cut, at] = term(1, i, half, at, first, size).astype(short)
-
-        by_columns(make)
+            term_out[i, rows_of, at] = term(1, i, half, at).astype(short)
+
+        if n < 2:
+            make(columns_of)
+        else:
+            by_columns(make)
         term_copies[i, n] = remote(
-            term_out.at[i, cut], term_in.at[i, cut],
+            term_out.at[i, rows_of, columns_of], term_in.at[i, rows_of, columns_of],
             term_send.at[0], term_recv.at[len(cuts) * i + n], weight_mate,
         )
 
@@ -515,7 +518,7 @@
         out = (grad_gate, grad_up, grad_down)[i]
         for n, cut in enumerate(cuts):
             term_copies[i, n].wait_recv()
-            out[cut, :] = (term_own[i, cut, :] + wide(term_in[i, cut, :])).astype(short)
+            out[cut] = (term_own[(i, *cut)] + wide(term_in[(i, *cut)])).astype(short)
 
     def expert_dx(k, part_of, at):
         here = pl.ds(pl.multiple_of(part_of * half_rows, half_rows), half_rows)

time: 135 us -> 134 us (level)
  no operation moved by 1% of the time
where the time goes in v7:
time: 134 us
  Pallas kernels  133 us (99%)
    pallas_call x1, Pallas kernels, fast_body(): pl.pallas_call(expert_kernel, out_shape=(jax.ShapeDtypeStruct((token_coun...  131 us

profile of v7, /device:TPU:0, one launch (start us, length us, event | category | flops | bytes accessed | tf_op | source)
XLA Modules:
  0.0 134.3 jit_solution(14928307712093003599)
XLA Ops:
  0.6 131.3 %shard_map.102 = (bf16[128,1792]{1,0:T(8,128)(2,1)S(1)}, bf16[128,1792]{1,0:T(8,128)(2,1)S(1)}, bf16[128,1792]{1,0:T(8,128)(2,1)S(1)}, bf16[128,1792]{1,0:T(8,12...) custom-call(bf16[128,7168]{1,0:T(8,128)(2,1)} %tokens.1, ...), custom_call_target="tpu_custom_call" | custom-call | tf_op jit(solution)/shard_map/pallas_call | solution.py:738
  131.9 2.2 %shard_map.103 = (bf16[128,7168]{1,0:T(8,128)(2,1)}, bf16[256,1792]{1,0:T(8,128)(2,1)}, bf16[256,1792]{1,0:T(8,128)(2,1)}, bf16[256,1792]{1,0:T(8,128)(2,1)}) custom-call(bf16[128,1792]{1,0:T(8,128)(2,1)S(1)} %get-tuple-element.11.refs_0_, bf16[128,1792]{1,0:T(8,128)(2,1)S(1)} %get-tuple-element.12.refs_1_, bf16[128,1792]{1,0:T(8,128)(2,1)S(1)} %get-tuple-element.13.refs_2_, ...), custom_call_target="tpu_custom_call" | custom-call | tf_op jit(solution)/shard_map/pallas_call | solution.py:790
